TPU v7x, 128 devices: a whole 4x4x4 slice. The times are simulated.
128 devices in a mesh: lat: 8 (over x, core), lon: 16 (over y, z).
Axes of the slice: x: 4, y: 4, z: 4, core: 2. Of those that a mesh axis runs over, the one named last changes fastest.
Arguments:
- ensemble: bfloat16 [80, 8, 64, 2048], P(None, None, 'lat', 'lon'), may hold values from -6 to 6
- static_sigma: float32 [8], replicated, may hold values from 0.5 to 2
- lat_taps: float32 [17], replicated, may hold values from 0.01 to 0.12
- lon_taps: float32 [17], replicated, may hold values from 0.01 to 0.12
- step_len: float32 [2], replicated, may hold values from 0.2 to 0.6
- send_cols: int32 [8, 16, 128, 64], P('lat', 'lon'), may hold values from 0 to 1023
- send_count: int32 [8, 16, 128], P('lat', 'lon'), may hold values from 32 to 64, as said below
- obs_ref: int32 [8, 16, 4, 2048], P('lat', 'lon'), may hold values from 0 to 8191, as said below
- obs_level: int32 [8, 16, 2048], P('lat', 'lon'), may hold values from 0 to 7
- obs_weight: float32 [8, 16, 4, 2048], P('lat', 'lon'), may hold values from 0 to 1
- innovation: float32 [8, 16, 2048], P('lat', 'lon'), may hold values from -6 to 6
- obs_precision: float32 [8, 16, 2048], P('lat', 'lon'), may hold values from 0.25 to 1
Outputs:
- ens_control: float32 [80, 8, 64, 2048], P(None, None, 'lat', 'lon')
- static_control: float32 [8, 64, 2048], P(None, 'lat', 'lon')
- departures: float32 [8, 16, 2048], P('lat', 'lon')
Inputs may be any that keep to these rules, and one draw needn't show every extreme that they name: `send_count`: number of leading slots of send_cols[a, b, e] that are live. One device receives 64 live slots from every device. `obs_ref`: position in the owning device's list L_e of received live columns; always below the total live slots that device receives.
All inputs are finite; a program needn't handle non-finite values.
Results may differ from a plain program's by a relative error of at most 0.0003.
Values may be sent and summed in bfloat16 or wider, within the bound.
No kernel may reach another device: no remote copies, remote signals or barrier semaphores. Data moves between devices by JAX's collectives and lax.ppermute only.
A program may use at most 128 MiB of HBM per device.

v0:
```python
import math

import jax
import jax.numpy as jnp
from jax import lax
from jax.experimental import pallas as pl
from jax.experimental.pallas import tpu as pltpu
from jax.sharding import PartitionSpec as P


HYBRID_STATIC = 0.5
HYBRID_ENSEMBLE = 0.8660254037844386
F32 = jnp.float32
BF16 = jnp.bfloat16
I32 = jnp.int32

MEM = 80
LEV = 8
ROWS = 8
LANES = 128
NOBS = 2048
SLOT = 64
DEV = 128
NLAT = 64
HW = 8
TAPS = 17
EDGE = 16
BUF = DEV * 4

VMEM = pltpu.VMEM
ARB = ("arbitrary",)


def whole(memory_space=VMEM):
    return pl.BlockSpec(memory_space=memory_space)


def split(value):
    high = value.astype(BF16).astype(F32)
    return high, value - high


def iota(shape, dim):
    return lax.broadcasted_iota(I32, shape, dim)


def nn(a, b):
    return lax.dot_general(a, b, (((1,), (0,)), ((), ())), preferred_element_type=F32)


def nt(a, b):
    return lax.dot_general(a, b, (((1,), (1,)), ((), ())), preferred_element_type=F32)


def matrices_kernel(band_ref, lat_ref, lon_ref, lat_mid, lon_mid, lat_fin, lon_fin):
    base = band_ref[0] * ROWS

    def pick(index, taps):
        out = jnp.zeros(index.shape, F32)
        for t in range(TAPS):
            out = jnp.where(index == t, taps[t], out)
        return out

    row = iota((8, 160), 0)
    col = iota((8, 160), 1)
    group = sum((col >= 40 * n).astype(I32) for n in range(1, 4))
    offset = col - 40 * group
    diff = row - offset + 2 * HW
    source = base - 2 * HW + offset
    total = jnp.zeros((8, 160), F32)
    for t in range(TAPS):
        middle = base + row + t - HW
        valid = jnp.logical_and(middle >= 0, middle < NLAT)
        total = total + jnp.where(valid, lat_ref[t] * pick(diff + t, lat_ref), 0.0)
    total = jnp.where(jnp.logical_and(source >= 0, source < NLAT), total, 0.0)
    high, low = split(total)
    blocks = []
    for s in range(2):
        blocks.append(jnp.where((group & 1) == s, high, 0.0))
        blocks.append(jnp.where(group == s, low, 0.0))
    lat_mid[...] = jnp.concatenate(blocks, axis=0).astype(BF16)

    row = iota((8, 192), 0)
    col = iota((8, 192), 1)
    group = sum((col >= 24 * n).astype(I32) for n in range(1, 8))
    offset = col - 24 * group
    source = base - HW + offset
    total = pick(row - offset + 2 * HW, lat_ref)
    total = jnp.where(jnp.logical_and(source >= 0, source < NLAT), total, 0.0)
    high, low = split(total)
    blocks = []
    for s in range(4):
        blocks.append(jnp.where((group & 3) == s, high, 0.0))
        blocks.append(jnp.where(group == s, low, 0.0))
    lat_fin[...] = jnp.concatenate(blocks, axis=0).astype(BF16)

    lag = iota((8, LANES), 1) - 2 * HW
    auto = jnp.zeros((8, LANES), F32)
    for t in range(TAPS):
        auto = auto + lon_ref[t] * pick(lag + t, lon_ref)

    def auto_at(n):
        return jnp.sum(jnp.where(lag[:1] == n, auto[:1], 0.0), axis=1, keepdims=True)

    coefficients = [auto_at(n) for n in range(2 * HW + 1)]
    main = iota((LANES, LANES), 0) - iota((LANES, LANES), 1)
    edge = iota((32, LANES), 0)
    edge = jnp.where(edge < EDGE, edge - EDGE, edge + LANES - EDGE) - iota((32, LANES), 1)

    def smooth_twice(distance):
        distance = jnp.abs(distance)
        out = jnp.zeros(distance.shape, F32)
        for n in range(2 * HW + 1):
            out = jnp.where(distance == n, coefficients[n], out)
        return out

    def place(out_ref, main_value, edge_value):
        main_high, main_low = split(main_value)
        edge_high, edge_low = split(edge_value)
        for v in range(4):
            out_ref[v, :LANES, :LANES] = main_high.astype(BF16)
            out_ref[v, :LANES, LANES:] = main_low.astype(BF16)
            out_ref[v, LANES:, :] = jnp.zeros((LANES, 2 * LANES), BF16)
            out_ref[v, LANES + 32 * v : LANES + 32 * (v + 1), :LANES] = edge_high.astype(BF16)
            out_ref[v, LANES + 32 * v : LANES + 32 * (v + 1), LANES:] = edge_low.astype(BF16)

    place(lon_mid, smooth_twice(main), smooth_twice(edge))
    place(lon_fin, pick(HW - main, lon_ref), pick(HW - edge, lon_ref))


def matrices(band, lat_taps, lon_taps):
    smem = whole(pltpu.SMEM)
    return pl.pallas_call(
        matrices_kernel,
        out_shape=(
            jax.ShapeDtypeStruct((32, 160), BF16),
            jax.ShapeDtypeStruct((4, 256, 256), BF16),
            jax.ShapeDtypeStruct((64, 192), BF16),
            jax.ShapeDtypeStruct((4, 256, 256), BF16),
        ),
        in_specs=[smem] * 3,
        out_specs=(whole(),) * 4,
        cost_estimate=pl.CostEstimate(flops=4000000, bytes_accessed=1100000, transcendentals=0),
        name="matrices",
    )(band, lat_taps, lon_taps)


def pack_kernel(e_ref, out_ref):
    row = iota((LANES, LANES), 0)
    col = iota((LANES, LANES), 1)
    inner = col & 31
    source = jnp.where(inner < EDGE, inner + LANES - EDGE, inner - EDGE)
    count = e_ref.shape[0]
    for g in range(2):
        total = None
        for v in range(4):
            choose = jnp.logical_and(row == source, (col >> 5) == v)
            choose = jnp.where(choose, 1.0, 0.0).astype(BF16)
            tile = e_ref[:, 4 * g + v].astype(F32).reshape(count * ROWS, LANES).astype(BF16)
            part = nn(tile, choose)
            total = part if total is None else total + part
        out_ref[:, g] = total.reshape(count, ROWS, LANES).astype(BF16)


def pack(ensemble):
    step = 16
    return pl.pallas_call(
        pack_kernel,
        grid=(MEM // step,),
        out_shape=jax.ShapeDtypeStruct((MEM, 2, ROWS, LANES), BF16),
        in_specs=[pl.BlockSpec((step, LEV, ROWS, LANES), lambda i: (i, 0, 0, 0))],
        out_specs=pl.BlockSpec((step, 2, ROWS, LANES), lambda i: (i, 0, 0, 0)),
        compiler_params=pltpu.CompilerParams(dimension_semantics=ARB),
        cost_estimate=pl.CostEstimate(flops=4000000, bytes_accessed=1600000, transcendentals=0),
        name="pack",
    )(ensemble)


CHUNK = 256
UNROLL = 2


def place_values(acc_ref, row_hot, lane_of, value_of, lane_iota):
    parts_high, parts_low = [], []
    for q in range(4):
        hit = lane_iota == lane_of[q]
        high, low = split(value_of[q])
        parts_high.append(jnp.where(hit, high, 0.0).astype(BF16))
        parts_low.append(jnp.where(hit, low, 0.0).astype(BF16))
    values = jnp.concatenate(
        [jnp.concatenate(parts_high, axis=1), jnp.concatenate(parts_low, axis=1)], axis=0
    )
    acc_ref[...] += nt(row_hot, values)


def hot_rows(row_of, row_iota):
    parts = [jnp.where(row_iota == row_of[q], 1.0, 0.0).astype(BF16) for q in range(4)]
    return jnp.concatenate(parts, axis=1)


def first_kernel(
    count_ref, ref_ref, level_ref, weight_ref, precision_ref, innovation_ref,
    buffer_ref, row_ref, lane_ref, acc_ref,
):
    counts = count_ref[...].astype(F32)
    below = iota((DEV, DEV), 1) <= iota((DEV, DEV), 0)
    ends = nn(jnp.where(below, 1.0, 0.0).astype(BF16), counts.astype(BF16))
    counts = jnp.concatenate([counts] * (CHUNK // LANES), axis=1)
    ends = jnp.concatenate([ends] * (CHUNK // LANES), axis=1)
    acc_ref[...] = jnp.zeros_like(acc_ref)
    row_iota = iota((BUF, CHUNK), 0).astype(F32)
    lane_iota = iota((LANES, CHUNK), 0).astype(F32)

    @pl.loop(0, NOBS // CHUNK, unroll=UNROLL)
    def _(c):
        part = pl.ds(pl.multiple_of(c * CHUNK, CHUNK), CHUNK)
        level = level_ref[:, part]
        low_level = (level & 3).astype(F32)
        high_level = ((level >> 2) * SLOT).astype(F32)
        forced = -(precision_ref[:, part] * innovation_ref[:, part])
        rows, lanes, values = [], [], []
        for q in range(4):
            position = ref_ref[q : q + 1, part].astype(F32)
            passed = position >= ends
            source = jnp.sum(jnp.where(passed, 1.0, 0.0), axis=0, keepdims=True)
            start = jnp.sum(jnp.where(passed, counts, 0.0), axis=0, keepdims=True)
            rows.append(source * 4.0 + low_level)
            lanes.append(high_level + position - start)
            row_ref[q : q + 1, part] = rows[q]
            lane_ref[q : q + 1, part] = lanes[q]
            values.append(weight_ref[q : q + 1, part] * forced)
        place_values(acc_ref, hot_rows(rows, row_iota), lanes, values, lane_iota)

    buffer_ref[...] = acc_ref[:, :LANES] + acc_ref[:, LANES:]


def first(count, ref, level, weight, precision, innovation):
    return pl.pallas_call(
        first_kernel,
        out_shape=(
            jax.ShapeDtypeStruct((BUF, LANES), F32),
            jax.ShapeDtypeStruct((4, NOBS), F32),
            jax.ShapeDtypeStruct((4, NOBS), F32),
        ),
        in_specs=[whole()] * 6,
        out_specs=(whole(),) * 3,
        scratch_shapes=[VMEM((BUF, 2 * LANES), F32)],
        cost_estimate=pl.CostEstimate(flops=40000000, bytes_accessed=600000, transcendentals=0),
        name="first",
    )(count, ref, level, weight, precision, innovation)


def second_kernel(
    incoming_ref, row_ref, lane_ref, weight_ref, precision_ref, innovation_ref, coef_ref,
    buffer_ref, departure_ref, acc_ref,
):
    flipped = incoming_ref[...].T
    high, low = split(flipped)
    table = jnp.concatenate([high, low], axis=0).astype(BF16)
    acc_ref[...] = jnp.zeros_like(acc_ref)
    row_iota = iota((BUF, CHUNK), 0).astype(F32)
    lane_iota = iota((LANES, CHUNK), 0).astype(F32)
    earlier = coef_ref[3, :1, :1]
    later = coef_ref[4, :1, :1]

    @pl.loop(0, NOBS // CHUNK, unroll=UNROLL)
    def _(c):
        part = pl.ds(pl.multiple_of(c * CHUNK, CHUNK), CHUNK)
        rows = [row_ref[q : q + 1, part] for q in range(4)]
        lanes = [lane_ref[q : q + 1, part] for q in range(4)]
        weights = [weight_ref[q : q + 1, part] for q in range(4)]
        innovation = innovation_ref[:, part]
        row_hot = hot_rows(rows, row_iota)
        found = nn(table, row_hot)
        found = found[:LANES] + found[LANES:]
        departure = -innovation
        for q in range(4):
            column = found[:, q * CHUNK : (q + 1) * CHUNK]
            picked = jnp.sum(jnp.where(lane_iota == lanes[q], column, 0.0), axis=0, keepdims=True)
            departure = departure + weights[q] * picked
        departure_ref[:, part] = departure
        forced = precision_ref[:, part] * (later * departure - earlier * innovation)
        values = [weights[q] * forced for q in range(4)]
        place_values(acc_ref, row_hot, lanes, values, lane_iota)

    buffer_ref[...] = acc_ref[:, :LANES] + acc_ref[:, LANES:]


def second(incoming, rows, lanes, weight, precision, innovation, coefs):
    return pl.pallas_call(
        second_kernel,
        out_shape=(
            jax.ShapeDtypeStruct((BUF, LANES), F32),
            jax.ShapeDtypeStruct((1, NOBS), F32),
        ),
        in_specs=[whole()] * 7,
        out_specs=(whole(),) * 2,
        scratch_shapes=[VMEM((BUF, 2 * LANES), F32)],
        cost_estimate=pl.CostEstimate(flops=60000000, bytes_accessed=800000, transcendentals=0),
        name="second",
    )(incoming, rows, lanes, weight, precision, innovation, coefs)


def swap_quadrants(tile):
    sub = iota((8, LANES), 0) < 4
    lane = iota((8, LANES), 1) < SLOT
    moved = pltpu.roll(pltpu.roll(tile, 4, 0), SLOT, 1)
    return jnp.where(sub == lane, tile, moved)


PAIRS = DEV // 2
GROUP = 4


def columns_kernel(buffer_ref, cell_ref, out_ref, grid_ref):
    lane_iota = iota((LANES, LANES), 0)
    total = jnp.zeros((LANES, LANES), F32)
    for n in range(0, PAIRS, GROUP):
        values, hots = [], []
        for m in range(n, n + GROUP):
            tile = swap_quadrants(buffer_ref[8 * m : 8 * m + 8, :])
            cell = cell_ref[m : m + 1, :]
            row = cell >> 7
            high, low = split(tile)
            masks = [row == r for r in range(ROWS)]
            values.append(
                jnp.concatenate(
                    [jnp.where(k, high, 0.0) for k in masks] + [jnp.where(k, low, 0.0) for k in masks],
                    axis=0,
                ).astype(BF16)
            )
            hots.append(jnp.where(lane_iota == (cell & 127), 1.0, 0.0).astype(BF16))
        total = total + nt(jnp.concatenate(values, axis=1), jnp.concatenate(hots, axis=1))

    grid_ref[...] = total[:64] + total[64:]
    lane = iota((ROWS, LANES), 1)
    inner = lane & 31
    edges = [jnp.zeros((ROWS, LANES), F32)] * 2
    for l in range(LEV):
        tile = grid_ref[pl.ds(l, ROWS, stride=LEV), :]
        out_ref[l] = tile
        v = l % 4
        right = pltpu.roll(tile, (32 * v + EDGE) % LANES, 1)
        left = pltpu.roll(tile, (32 * v + EDGE) % LANES, 1)
        moved = jnp.where(inner < EDGE, right, left)
        edges[l // 4] = jnp.where((lane >> 5) == v, moved, edges[l // 4])
    out_ref[LEV] = edges[0]
    out_ref[LEV + 1] = edges[1]


def columns(buffer, cells):
    return pl.pallas_call(
        columns_kernel,
        out_shape=jax.ShapeDtypeStruct((LEV + 2, ROWS, LANES), F32),
        in_specs=[whole()] * 2,
        out_specs=whole(),
        scratch_shapes=[VMEM((64, LANES), F32)],
        cost_estimate=pl.CostEstimate(flops=20000000, bytes_accessed=400000, transcendentals=0),
        name="columns",
    )(buffer, cells)


def slots_kernel(increment_ref, cell_ref, out_ref):
    rows = [increment_ref[pl.ds(r, LEV, stride=ROWS), :] for r in range(ROWS)]
    pairs = [split(value) for value in rows]
    table = jnp.concatenate([p[0] for p in pairs] + [p[1] for p in pairs], axis=0).astype(BF16)
    lane_iota = iota((LANES, LANES), 0)

    for n in range(0, PAIRS, GROUP):
        hots, cells = [], []
        for m in range(n, n + GROUP):
            cell = cell_ref[m : m + 1, :]
            cells.append(cell >> 7)
            hots.append(jnp.where(lane_iota == (cell & 127), 1.0, 0.0).astype(BF16))
        found = nn(table, jnp.concatenate(hots, axis=1))
        found = found[:64] + found[64:]
        for g in range(GROUP):
            tile = jnp.zeros((LEV, LANES), F32)
            for r in range(ROWS):
                part = found[8 * r : 8 * r + 8, g * LANES : (g + 1) * LANES]
                tile = jnp.where(cells[g] == r, part, tile)
            out_ref[8 * (n + g) : 8 * (n + g) + 8, :] = swap_quadrants(tile)


def slots(increment, cells):
    return pl.pallas_call(
        slots_kernel,
        out_shape=jax.ShapeDtypeStruct((BUF, LANES), F32),
        in_specs=[whole()] * 2,
        out_specs=whole(),
        cost_estimate=pl.CostEstimate(flops=20000000, bytes_accessed=400000, transcendentals=0),
        name="slots",
    )(increment, cells)


def row_pass(e_refs, fields, lat_ref, stack, out_ref, lane0):
    per = MEM // stack
    wide = 2
    lat = lat_ref[...]

    def column_of(tiles):
        value = jnp.concatenate(tiles, axis=0)
        high = value.astype(BF16)
        low = (value - high.astype(F32)).astype(BF16)
        return jnp.concatenate([high, low], axis=0)

    def store(row, value):
        high = value.astype(BF16)
        out_ref[0, row : row + 16, lane0 : lane0 + LANES] = high
        low = (value - high.astype(F32)).astype(BF16)
        out_ref[1, row : row + 16, lane0 : lane0 + LANES] = low

    def block(value, s, n):
        tile = value[16 * s : 16 * s + 16, n * LANES : (n + 1) * LANES]
        return tile[:8] + tile[8:]

    for c in range(0, per, wide):
        parts = []
        for n in range(c, c + wide):
            tiles = []
            for s in range(stack):
                tiles += [e[s * per + n, 0].astype(F32) * f for e, f in zip(e_refs, fields)]
            parts.append(column_of(tiles))
        value = nn(lat, jnp.concatenate(parts, axis=1))
        for s in range(stack):
            for n in range(0, wide, 2):
                pair = jnp.concatenate([block(value, s, n), block(value, s, n + 1)], axis=0)
                store((s * per + c + n) * 8, pair)

    blank = [jnp.zeros((ROWS, LANES), F32)] * (len(fields) * (stack - 1))
    one = block(nn(lat, column_of(list(fields) + blank)), 0, 0)
    store(MEM * 8, jnp.concatenate([one, jnp.zeros_like(one)], axis=0))


def column_pass(in_ref, weights, start, size):
    value = nn(in_ref[0, start : start + size, :], weights)
    value = value + nn(in_ref[1, start : start + size, :], weights)
    return value[:, :LANES] + value[:, LANES:]


def merge_edges(left, right):
    inner = iota((ROWS, LANES), 1) & 31
    return jnp.where(inner < EDGE, left, right)


def middle_kernel(*refs):
    e_refs = refs[:5]
    h_refs = refs[5:10]
    f_refs = refs[10:15]
    left_ref, right_ref, lat_ref, lon_ref, coef_ref, out_ref, pass_ref = refs[15:]
    l = pl.program_id(0)

    @pl.when((l & 3) == 0)
    def _():
        g = l >> 2
        fields = [merge_edges(left_ref[x, g], right_ref[x, g]) for x in range(5)]
        row_pass(h_refs, fields, lat_ref, 2, pass_ref, LANES)

    fields = [f_refs[x][l] for x in range(5)]
    row_pass(e_refs, fields, lat_ref, 2, pass_ref, 0)
    weights = lon_ref[0]
    step = 16

    total = jnp.zeros((ROWS, LANES), F32)
    for c in range(MEM // step):
        value = column_pass(pass_ref, weights, c * 8 * step, 8 * step)
        for k in range(step):
            own = e_refs[2][c * step + k, 0].astype(F32)
            total = total + value[8 * k : 8 * k + 8] * own
    single = column_pass(pass_ref, weights, MEM * 8, 16)[:8]
    out_ref[0] = coef_ref[0] * total + coef_ref[1, pl.ds(l, 1), :] * single


def level_block(count):
    return pl.BlockSpec((count, 1, ROWS, LANES), lambda l: (0, l, 0, 0))


def edge_block(count):
    return pl.BlockSpec((count, 1, ROWS, LANES), lambda l: (0, l // 4, 0, 0))


def middle(members, halos, fields, left, right, lat_mid, lon_mid, coefs):
    return pl.pallas_call(
        middle_kernel,
        grid=(LEV,),
        out_shape=jax.ShapeDtypeStruct((LEV, ROWS, LANES), F32),
        in_specs=[level_block(MEM)] * 5
        + [edge_block(MEM)] * 5
        + [whole()] * 8
        + [pl.BlockSpec((1, 256, 256), lambda l: (l % 4, 0, 0)), whole()],
        out_specs=pl.BlockSpec((1, ROWS, LANES), lambda l: (l, 0, 0)),
        scratch_shapes=[VMEM((2, MEM * 8 + 16, 256), BF16)],
        compiler_params=pltpu.CompilerParams(dimension_semantics=ARB),
        cost_estimate=pl.CostEstimate(flops=100000000, bytes_accessed=9000000, transcendentals=0),
        name="middle",
    )(*members, *halos, *fields, left, right, lat_mid, lon_mid, coefs)


def final_kernel(*refs):
    e_refs = refs[:3]
    h_refs = refs[3:6]
    f_refs = refs[6:9]
    left_ref, right_ref, lat_ref, lon_ref, coef_ref, out_ref, static_ref, pass_ref = refs[9:]
    l = pl.program_id(0)

    @pl.when((l & 3) == 0)
    def _():
        g = l >> 2
        fields = [merge_edges(left_ref[x, g], right_ref[x, g]) for x in range(3)]
        row_pass(h_refs, fields, lat_ref, 4, pass_ref, LANES)

    fields = [f_refs[x][l] for x in range(3)]
    row_pass(e_refs, fields, lat_ref, 4, pass_ref, 0)
    weights = lon_ref[0]
    step = 16
    scale = -HYBRID_ENSEMBLE / math.sqrt(MEM - 1)

    for c in range(MEM // step):
        value = column_pass(pass_ref, weights, c * 8 * step, 8 * step)
        out_ref[c * step : (c + 1) * step, 0] = (scale * value).reshape(step, ROWS, LANES)

    single = column_pass(pass_ref, weights, MEM * 8, 16)[:8]
    static_ref[0] = coef_ref[2, pl.ds(l, 1), :] * single


def final(members, halos, fields, left, right, lat_fin, lon_fin, coefs):
    return pl.pallas_call(
        final_kernel,
        grid=(LEV,),
        out_shape=(
            jax.ShapeDtypeStruct((MEM, LEV, ROWS, LANES), F32),
            jax.ShapeDtypeStruct((LEV, ROWS, LANES), F32),
        ),
        in_specs=[level_block(MEM)] * 3
        + [edge_block(MEM)] * 3
        + [whole()] * 6
        + [pl.BlockSpec((1, 256, 256), lambda l: (l % 4, 0, 0)), whole()],
        out_specs=(level_block(MEM), pl.BlockSpec((1, ROWS, LANES), lambda l: (l, 0, 0))),
        scratch_shapes=[VMEM((2, MEM * 8 + 16, 256), BF16)],
        compiler_params=pltpu.CompilerParams(dimension_semantics=ARB),
        cost_estimate=pl.CostEstimate(flops=100000000, bytes_accessed=9000000, transcendentals=0),
        name="final",
    )(*members, *halos, *fields, left, right, lat_fin, lon_fin, coefs)


def shift(value, axis, step):
    count = lax.axis_size(axis)
    return lax.ppermute(value, axis, [(i, (i + step) % count) for i in range(count)])


def edges_kernel(*refs):
    for x, ref in enumerate(refs[:-1]):
        refs[-1][x] = ref[LEV:]


def surround(forcing, reach):
    bands = range(reach, -reach - 1, -1)
    fields = [shift(forcing, "lat", d) if d else forcing for d in bands]
    edges = pl.pallas_call(
        edges_kernel,
        out_shape=jax.ShapeDtypeStruct((len(fields), 2, ROWS, LANES), F32),
        in_specs=[whole()] * len(fields),
        out_specs=whole(),
        cost_estimate=pl.CostEstimate(flops=100000, bytes_accessed=100000, transcendentals=0),
        name="edges",
    )(*fields)
    return fields, shift(edges, "lon", 1), shift(edges, "lon", -1)


def route(buffer):
    buffer = buffer.reshape(DEV, 4, LANES)
    out = lax.all_to_all(buffer, ("lat", "lon"), split_axis=0, concat_axis=0, tiled=True)
    return out.reshape(BUF, LANES)


def per_device(
    ensemble,
    static_sigma,
    lat_taps,
    lon_taps,
    step_len,
    send_cols,
    send_count,
    obs_ref,
    obs_level,
    obs_weight,
    innovation,
    obs_precision,
):
    ens_scale = HYBRID_ENSEMBLE / math.sqrt(MEM - 1)
    counts = jnp.broadcast_to(send_count.reshape(DEV, 1, 1), (DEV, 1, LANES))
    received = lax.all_to_all(counts, ("lat", "lon"), split_axis=0, concat_axis=0, tiled=True)
    received = received.reshape(DEV, LANES)
    cells = send_cols.reshape(PAIRS, LANES)
    level = obs_level.reshape(1, NOBS)
    ref = obs_ref.reshape(4, NOBS)
    weight = obs_weight.reshape(4, NOBS)
    innov = innovation.reshape(1, NOBS)
    precision = obs_precision.reshape(1, NOBS)

    ones = jnp.ones((LEV, LANES), F32)
    sigma = static_sigma[:, None] * ones
    coefs = jnp.stack(
        [
            (-step_len[0] * ens_scale * ens_scale) * ones,
            (-step_len[0] * HYBRID_STATIC * HYBRID_STATIC) * sigma * sigma,
            -HYBRID_STATIC * sigma,
            ((1.0 - step_len[1]) * step_len[0]) * ones,
            step_len[1] * ones,
        ]
    )
    band = lax.axis_index("lat").astype(I32).reshape(1)
    lat_mid, lon_mid, lat_fin, lon_fin = matrices(band, lat_taps, lon_taps)

    north = shift(ensemble, "lat", 1)
    south = shift(ensemble, "lat", -1)
    packed = pack(ensemble)
    from_left = shift(packed, "lon", 1)
    from_right = shift(packed, "lon", -1)
    inner = lax.broadcasted_iota(I32, packed.shape, 3) & 31
    halo = jnp.where(inner < EDGE, from_left, from_right)
    north2 = shift(north, "lat", 1)
    south2 = shift(south, "lat", -1)
    halo_n = shift(halo, "lat", 1)
    halo_s = shift(halo, "lat", -1)
    halo_n2 = shift(halo_n, "lat", 1)
    halo_s2 = shift(halo_s, "lat", -1)
    members = [north2, north, ensemble, south, south2]
    halos = [halo_n2, halo_n, halo, halo_s, halo_s2]

    outgoing, rows, lanes = first(received, ref, level, weight, precision, innov)
    arrived = route(outgoing)
    forcing = columns(arrived, cells)
    around = surround(forcing, 2)
    increment = middle(members, halos, *around, lat_mid, lon_mid, coefs)
    incoming = route(slots(increment.reshape(LEV * ROWS, LANES), cells))
    outgoing, departure = second(incoming, rows, lanes, weight, precision, innov, coefs)
    around = surround(columns(route(outgoing), cells), 1)
    control, static = final(members[1:4], halos[1:4], *around, lat_fin, lon_fin, coefs)
    return (control, static, departure.reshape(1, 1, -1))


def solution(mesh):
    return jax.shard_map(
        per_device,
        mesh=mesh,
        in_specs=(
            P(None, None, "lat", "lon"),
            P(),
            P(),
            P(),
            P(),
            P("lat", "lon", None, None),
            P("lat", "lon", None),
            P("lat", "lon", None, None),
            P("lat", "lon", None),
            P("lat", "lon", None, None),
            P("lat", "lon", None),
            P("lat", "lon", None),
        ),
        out_specs=(P(None, None, "lat", "lon"), P(None, "lat", "lon"), P("lat", "lon", None)),
        check_vma=False,
    )
```

profile of v0, /device:TPU:0, one launch (start us, length us, event | category | flops | bytes accessed | tf_op | source)
XLA Modules:
  0.0 182.8 jit_solution(13820083418328264039)
XLA Ops:
  0.7 2.3 %collective-permute-start.1 = (bf16[80,8,8,128]{3,2,1,0:T(8,128)(2,1)}, bf16[80,8,8,128]{3,2,1,0:T(8,128)(2,1)S(1)}, u32[]{:S(2)}, u32[]{:S(2)}) collective-permute-start(bf16[80,8,8,128]{3,2,1,0:T(8,128)(2,1)} %refs_1_.1), channel_id=1, source_target_pairs={{0,112},{16,0},{32,16},{48,32},{64,48},{80,64},{96,80},{112,96},{1... | collective-permute-start | bytes 3932168 | tf_op jit(solution)/shard_map/ppermute | solution.py:548
  3.0 0.0 collective-permute-start
  3.0 4.3 %pack.1 = bf16[80,2,8,128]{3,2,1,0:T(8,128)(2,1)} custom-call(bf16[80,8,8,128]{3,2,1,0:T(8,128)(2,1)} %refs_1_.1), custom_call_target="tpu_custom_call" | custom-call | flops 4000000 | bytes 1600000 | tf_op jit(solution)/shard_map/pack/pallas_call | solution.py:167
  7.3 6.5 %collective-permute-start.3 = (bf16[80,2,8,128]{3,2,1,0:T(8,128)(2,1)}, bf16[80,2,8,128]{3,2,1,0:T(8,128)(2,1)S(1)}, u32[]{:S(2)}, u32[]{:S(2)}) collective-permute-start(bf16[80,2,8,128]{3,2,1,0:T(8,128)(2,1)} %pack.1), channel_id=1, source_target_pairs={{0,15},{1,0},{2,1},{3,2},{4,3},{5,4},{6,5},{7,6},{8,7},{9,8},{10,9... | collective-permute-start | bytes 983048 | tf_op jit(solution)/shard_map/ppermute | solution.py:548
  13.8 0.8 broadcast_in_dim.9
  14.6 9.1 %all-to-all-start = ((s32[128,1,128]{2,1,0:T(1,128)}), s32[128,1,128]{2,1,0:T(1,128)S(1)}, u32[]{:S(2)}, u32[]{:S(2)}) async-start(s32[128,1,128]{2,1,0:T(1,128)} %broadcast_in_dim.9), calls=%async_computation | async-start | bytes 131072 | tf_op jit(solution)/shard_map/all_to_all | solution.py:592
  23.7 0.6 fusion
  24.3 8.9 %all-to-all-done = s32[128,1,128]{2,1,0:T(1,128)S(1)} async-done(((s32[128,1,128]{2,1,0:T(1,128)}), s32[128,1,128]{2,1,0:T(1,128)S(1)}, u32[]{:S(2)}, u32[]{:S(2)}) %all-to-all-start) | async-done | bytes 65568 | tf_op jit(solution)/shard_map/all_to_all | solution.py:592
  33.2 0.6 copy-done.5
  33.8 5.7 %first.1 = (f32[512,128]{1,0:T(8,128)}, f32[4,2048]{1,0:T(4,128)}, f32[4,2048]{1,0:T(4,128)}) custom-call(s32[128,128]{1,0:T(8,128)} %bitcast.26, s32[4,2048]{1,0:T(4,128)} %bitcast.30, s32[1,2048]{1,0:T(1,128)} %bitcast.35, f32[4,2048]{1,0:T(4,128)} %bitcast.28, f32[1,2048]{1,0:T(1,128)} %bitcast.31, f32[1,2048]{1,0:T(1,128)} %bitcast.33), custom_call_target="tpu_custom_call" | custom-call | flops 40000000 | bytes 600000 | tf_op jit(solution)/shard_map/first/pallas_call | solution.py:238
  39.5 4.6 %all-to-all-start.1 = ((f32[128,4,128]{2,1,0:T(4,128)}), f32[128,4,128]{2,1,0:T(4,128)S(1)}, u32[]{:S(2)}, u32[]{:S(2)}) async-start(f32[128,4,128]{2,1,0:T(4,128)} %bitcast.24), calls=%async_computation.1 | async-start | bytes 524288 | tf_op jit(solution)/shard_map/all_to_all | solution.py:572
  44.1 0.0 collective-permute-done.1.refs_3_.refs_2_
  44.2 1.9 %collective-permute-start.7 = (bf16[80,8,8,128]{3,2,1,0:T(8,128)(2,1)S(1)}, bf16[80,8,8,128]{3,2,1,0:T(8,128)(2,1)}, u32[]{:S(2)}, u32[]{:S(2)}) collective-permute-start(bf16[80,8,8,128]{3,2,1,0:T(8,128)(2,1)S(1)} %collective-permute-done.1.refs_3_.refs_2_), channel_id=1, source_target_pairs={{0,112},{16,0},{32,16},{48,32},{64,48},{80,64},{96,80},{112,96},{1... | collective-permute-start | bytes 3932168 | tf_op jit(solution)/shard_map/ppermute | solution.py:548
  46.1 0.0 collective-permute-done.refs_1_.refs_0_
  46.1 0.0 collective-permute-start.6
  46.7 0.1 copy.17
  46.8 0.7 reshape.67.cell_ref
  47.5 7.8 %all-to-all-done.1 = f32[128,4,128]{2,1,0:T(4,128)S(1)} async-done(((f32[128,4,128]{2,1,0:T(4,128)}), f32[128,4,128]{2,1,0:T(4,128)S(1)}, u32[]{:S(2)}, u32[]{:S(2)}) %all-to-all-start.1) | async-done | bytes 262176 | tf_op jit(solution)/shard_map/all_to_all | solution.py:572
  55.3 0.7 copy-done.4
  56.0 2.8 %columns.2.refs_2_.refs_12_ = f32[10,8,128]{2,1,0:T(8,128)} custom-call(f32[512,128]{1,0:T(8,128)} %bitcast.21, s32[64,128]{1,0:T(8,128)} %reshape.67.cell_ref), custom_call_target="tpu_custom_call" | custom-call | flops 20000000 | bytes 400000 | tf_op jit(solution)/shard_map/columns/pallas_call | solution.py:352
  58.8 0.9 collective-permute-start.13
  59.7 1.0 broadcast_select_fusion.refs_7_.refs_4_
  60.7 0.3 collective-permute-start.5
  61.0 2.1 %collective-permute-done.13.refs_4_.refs_14_ = f32[10,8,128]{2,1,0:T(8,128)S(1)} collective-permute-done((f32[10,8,128]{2,1,0:T(8,128)}, f32[10,8,128]{2,1,0:T(8,128)S(1)}, u32[]{:S(2)}, u32[]{:S(2)}) %collective-permute-start.13) | collective-permute-done | bytes 40992 | tf_op jit(solution)/shard_map/ppermute | solution.py:548
  63.1 0.0 collective-permute-start.4
  63.1 0.0 collective-permute-done.12.refs_3_.refs_13_
  63.2 1.6 collective-permute-start.11
  64.8 0.1 constant_dynamic-update-slice_fusion.3
  64.8 6.4 %collective-permute-done.11.refs_1_.refs_11_ = f32[10,8,128]{2,1,0:T(8,128)S(1)} collective-permute-done((f32[10,8,128]{2,1,0:T(8,128)}, f32[10,8,128]{2,1,0:T(8,128)S(1)}, u32[]{:S(2)}, u32[]{:S(2)}) %collective-permute-start.11) | collective-permute-done | bytes 40992 | tf_op jit(solution)/shard_map/ppermute | solution.py:548
  71.3 0.3 collective-permute-start.10
  71.6 0.3 collective-permute-start.9
  71.9 0.0 collective-permute-done.4.refs_6_.refs_3_
  71.9 0.2 collective-permute-start.8
  72.1 0.1 constant_dynamic-update-slice_fusion.2
  73.5 3.6 %collective-permute-done.10.refs_0_.refs_10_ = f32[10,8,128]{2,1,0:T(8,128)S(1)} collective-permute-done((f32[10,8,128]{2,1,0:T(8,128)}, f32[10,8,128]{2,1,0:T(8,128)S(1)}, u32[]{:S(2)}, u32[]{:S(2)}) %collective-permute-start.10) | collective-permute-done | bytes 40992 | tf_op jit(solution)/shard_map/ppermute | solution.py:548
  77.1 0.6 copy-done.12
  77.7 1.5 edges.2
  79.2 5.6 %collective-permute-start.15 = (f32[5,2,8,128]{3,2,1,0:T(8,128)}, f32[5,2,8,128]{3,2,1,0:T(8,128)S(1)}, u32[]{:S(2)}, u32[]{:S(2)}) collective-permute-start(f32[5,2,8,128]{3,2,1,0:T(8,128)} %edges.2), channel_id=1, source_target_pairs={{0,15},{1,0},{2,1},{3,2},{4,3},{5,4},{6,5},{7,6},{8,7},{9,8},{10,9... | collective-permute-start | bytes 122888 | tf_op jit(solution)/shard_map/ppermute | solution.py:548
  84.8 2.0 %collective-permute-done.15.refs_16_ = f32[5,2,8,128]{3,2,1,0:T(8,128)S(1)} collective-permute-done((f32[5,2,8,128]{3,2,1,0:T(8,128)}, f32[5,2,8,128]{3,2,1,0:T(8,128)S(1)}, u32[]{:S(2)}, u32[]{:S(2)}) %collective-permute-start.15) | collective-permute-done | bytes 40992 | tf_op jit(solution)/shard_map/ppermute | solution.py:548
  86.8 0.7 constant_dynamic-update-slice_fusion.refs_19_.coef_ref.refs_13_
  87.5 2.1 %matrices.1 = (bf16[32,160]{1,0:T(8,128)(2,1)}, bf16[4,256,256]{2,1,0:T(8,128)(2,1)}, bf16[64,192]{1,0:T(8,128)(2,1)}, bf16[4,256,256]{2,1,0:T(8,128)(2,1)}) custom-call(s32[1]{0:T(128)} %bitcast.9.band_ref, f32[17]{0:T(128)} %lat_ref.1, f32[17]{0:T(128)} %lon_ref.1), custom_call_target="tpu_custom_call" | custom-call | flops 4000000 | bytes 1100000 | tf_op jit(solution)/shard_map/matrices/pallas_call | solution.py:133
  89.6 4.9 %collective-permute-done.14.refs_15_ = f32[5,2,8,128]{3,2,1,0:T(8,128)S(1)} collective-permute-done((f32[5,2,8,128]{3,2,1,0:T(8,128)}, f32[5,2,8,128]{3,2,1,0:T(8,128)S(1)}, u32[]{:S(2)}, u32[]{:S(2)}) %collective-permute-start.14) | collective-permute-done | bytes 40992 | tf_op jit(solution)/shard_map/ppermute | solution.py:548
  94.6 0.0 collective-permute-done.9.refs_9_
  94.6 0.0 collective-permute-done.8.refs_5_
  94.6 0.0 collective-permute-done.6.refs_0_
  94.6 0.5 copy-done.14
  95.2 11.5 %middle.1 = f32[8,8,128]{2,1,0:T(8,128)} custom-call(bf16[80,8,8,128]{3,2,1,0:T(8,128)(2,1)} %collective-permute-done.6.refs_0_, bf16[80,8,8,128]{3,2,1,0:T(8,128)(2,1)} %copy-done.1, bf16[80,8,8,128]{3,2,1,0:T(8,128)(2,1)} %refs_1_.1, bf16[80,8,8,128]{3,2,1,0:T(8,128)(2,1)} %copy-done, bf16[80,8,8,128]{3,2,1,0:T(8,128)(2,1)} %collective-permute-done.7.refs_4_, ...), custom_call_target="tpu_custom_call" | custom-call | flops 100000000 | bytes 9000000 | tf_op jit(solution)/shard_map/middle/pallas_call | solution.py:483
  106.7 2.6 %slots.1 = f32[512,128]{1,0:T(8,128)} custom-call(f32[64,128]{1,0:T(8,128)} %bitcast.27, s32[64,128]{1,0:T(8,128)} %reshape.67.cell_ref), custom_call_target="tpu_custom_call" | custom-call | flops 20000000 | bytes 400000 | tf_op jit(solution)/shard_map/slots/pallas_call | solution.py:386
  109.3 16.4 %all_to_all.20 = f32[128,4,128]{2,1,0:T(4,128)} all-to-all(f32[128,4,128]{2,1,0:T(4,128)} %bitcast.20), channel_id=1, replica_groups=mesh['lat'=8,'lon'=16] {'lat','lon'}, dimensions={0} | all-to-all | bytes 524288 | tf_op jit(solution)/shard_map/all_to_all | solution.py:572
  125.7 10.8 %second.1 = (f32[512,128]{1,0:T(8,128)}, f32[1,2048]{1,0:T(1,128)}) custom-call(f32[512,128]{1,0:T(8,128)} %bitcast.22, f32[4,2048]{1,0:T(4,128)} %get-tuple-element.17.row_ref, f32[4,2048]{1,0:T(4,128)} %get-tuple-element.18.lane_ref, f32[4,2048]{1,0:T(4,128)} %bitcast.29, f32[1,2048]{1,0:T(1,128)} %bitcast.32, f32[1,2048]{1,0:T(1,128)} %bitcast.34, ...), custom_call_target="tpu_custom_call" | custom-call | flops 60000000 | bytes 800000 | tf_op jit(solution)/shard_map/second/pallas_call | solution.py:290
  136.5 16.6 %all_to_all.21 = f32[128,4,128]{2,1,0:T(4,128)} all-to-all(f32[128,4,128]{2,1,0:T(4,128)} %bitcast.25), channel_id=1, replica_groups=mesh['lat'=8,'lon'=16] {'lat','lon'}, dimensions={0} | all-to-all | bytes 524288 | tf_op jit(solution)/shard_map/all_to_all | solution.py:572
  153.1 2.8 %columns.3.refs_1_.refs_7_ = f32[10,8,128]{2,1,0:T(8,128)} custom-call(f32[512,128]{1,0:T(8,128)} %bitcast.23, s32[64,128]{1,0:T(8,128)} %reshape.67.cell_ref), custom_call_target="tpu_custom_call" | custom-call | flops 20000000 | bytes 400000 | tf_op jit(solution)/shard_map/columns/pallas_call | solution.py:352
  155.9 0.6 collective-permute-start.17
  156.5 0.0 collective-permute-start.16
  156.5 2.0 %collective-permute-done.17.refs_2_.refs_8_ = f32[10,8,128]{2,1,0:T(8,128)S(1)} collective-permute-done((f32[10,8,128]{2,1,0:T(8,128)}, f32[10,8,128]{2,1,0:T(8,128)S(1)}, u32[]{:S(2)}, u32[]{:S(2)}) %collective-permute-start.17) | collective-permute-done | bytes 40992 | tf_op jit(solution)/shard_map/ppermute | solution.py:548
  158.5 2.9 %collective-permute-done.16.refs_0_.refs_6_ = f32[10,8,128]{2,1,0:T(8,128)S(1)} collective-permute-done((f32[10,8,128]{2,1,0:T(8,128)}, f32[10,8,128]{2,1,0:T(8,128)S(1)}, u32[]{:S(2)}, u32[]{:S(2)}) %collective-permute-start.16) | collective-permute-done | bytes 40992 | tf_op jit(solution)/shard_map/ppermute | solution.py:548
  161.4 0.6 copy-done.8
  162.0 1.4 edges.3
  163.4 1.2 collective-permute-start.19
  164.6 0.8 collective-permute-start.18
  165.4 2.0 %collective-permute-done.19.refs_10_ = f32[3,2,8,128]{3,2,1,0:T(8,128)S(1)} collective-permute-done((f32[3,2,8,128]{3,2,1,0:T(8,128)}, f32[3,2,8,128]{3,2,1,0:T(8,128)S(1)}, u32[]{:S(2)}, u32[]{:S(2)}) %collective-permute-start.19) | collective-permute-done | bytes 24608 | tf_op jit(solution)/shard_map/ppermute | solution.py:548
  167.4 4.5 %collective-permute-done.18.refs_9_ = f32[3,2,8,128]{3,2,1,0:T(8,128)S(1)} collective-permute-done((f32[3,2,8,128]{3,2,1,0:T(8,128)}, f32[3,2,8,128]{3,2,1,0:T(8,128)S(1)}, u32[]{:S(2)}, u32[]{:S(2)}) %collective-permute-start.18) | collective-permute-done | bytes 24608 | tf_op jit(solution)/shard_map/ppermute | solution.py:548
  172.0 0.6 copy-done.17
  172.6 10.1 %final.1 = (f32[80,8,8,128]{3,2,1,0:T(8,128)}, f32[8,8,128]{2,1,0:T(8,128)}) custom-call(bf16[80,8,8,128]{3,2,1,0:T(8,128)(2,1)} %copy-done.1, bf16[80,8,8,128]{3,2,1,0:T(8,128)(2,1)} %refs_1_.1, bf16[80,8,8,128]{3,2,1,0:T(8,128)(2,1)} %copy-done, bf16[80,2,8,128]{3,2,1,0:T(8,128)(2,1)} %collective-permute-done.4.refs_6_.refs_3_, ...), custom_call_target="tpu_custom_call" | custom-call | flops 100000000 | bytes 9000000 | tf_op jit(solution)/shard_map/final/pallas_call | solution.py:527
  (47 shorter events, 0.1 us)
Async XLA Ops:
  0.6 13.1 %copy-start.19 = (s32[1,1,128]{2,1,0:T(1,128)S(1)}, s32[1,1,128]{2,1,0:T(1,128)}, u32[]{:S(2)}) copy-start(s32[1,1,128]{2,1,0:T(1,128)} %param.18) | copy-start | bytes 1540
  0.6 23.1 %copy-start.18 = (f32[2]{0:T(128)S(1)}, f32[2]{0:T(128)}, u32[]{:S(2)}) copy-start(f32[2]{0:T(128)} %param.16) | copy-start | bytes 28
  0.7 46.1 %copy-start.15 = (s32[1,1,128,64]{2,3,1,0:T(8,128)S(1)}, s32[1,1,128,64]{2,3,1,0:T(8,128)}, u32[]{:S(2)}) copy-start(s32[1,1,128,64]{2,3,1,0:T(8,128)} %param.17) | copy-start | bytes 98308
  0.7 46.8 %copy-start.20 = (f32[8]{0:T(128)S(1)}, f32[8]{0:T(128)}, u32[]{:S(2)}) copy-start(f32[8]{0:T(128)} %param.13) | copy-start | bytes 100
  0.7 43.5 %collective-permute-start.1 = (bf16[80,8,8,128]{3,2,1,0:T(8,128)(2,1)}, bf16[80,8,8,128]{3,2,1,0:T(8,128)(2,1)S(1)}, u32[]{:S(2)}, u32[]{:S(2)}) collective-permute-start(bf16[80,8,8,128]{3,2,1,0:T(8,128)(2,1)} %refs_1_.1), channel_id=1, source_target_pairs={{0,112},{16,0},{32,16},{48,32},{64,48},{80,64},{96,80},{112,96},{1... | collective-permute-start | bytes 3932168 | tf_op jit(solution)/shard_map/ppermute | solution.py:548
  3.0 43.1 %collective-permute-start = (bf16[80,8,8,128]{3,2,1,0:T(8,128)(2,1)}, bf16[80,8,8,128]{3,2,1,0:T(8,128)(2,1)S(1)}, u32[]{:S(2)}, u32[]{:S(2)}) collective-permute-start(bf16[80,8,8,128]{3,2,1,0:T(8,128)(2,1)} %refs_1_.1), channel_id=1, source_target_pairs={{0,16},{16,32},{32,48},{48,64},{64,80},{80,96},{96,112},{112,0},{1... | collective-permute-start | bytes 3932168 | tf_op jit(solution)/shard_map/ppermute | solution.py:548
  7.3 52.4 %collective-permute-start.3 = (bf16[80,2,8,128]{3,2,1,0:T(8,128)(2,1)}, bf16[80,2,8,128]{3,2,1,0:T(8,128)(2,1)S(1)}, u32[]{:S(2)}, u32[]{:S(2)}) collective-permute-start(bf16[80,2,8,128]{3,2,1,0:T(8,128)(2,1)} %pack.1), channel_id=1, source_target_pairs={{0,15},{1,0},{2,1},{3,2},{4,3},{5,4},{6,5},{7,6},{8,7},{9,8},{10,9... | collective-permute-start | bytes 983048 | tf_op jit(solution)/shard_map/ppermute | solution.py:548
  13.7 46.0 %collective-permute-start.2 = (bf16[80,2,8,128]{3,2,1,0:T(8,128)(2,1)}, bf16[80,2,8,128]{3,2,1,0:T(8,128)(2,1)}, u32[]{:S(2)}, u32[]{:S(2)}) collective-permute-start(bf16[80,2,8,128]{3,2,1,0:T(8,128)(2,1)} %pack.1), channel_id=1, source_target_pairs={{0,1},{1,2},{2,3},{3,4},{4,5},{5,6},{6,7},{7,8},{8,9},{9,10},{10,1... | collective-permute-start | bytes 983048 | tf_op jit(solution)/shard_map/ppermute | solution.py:548
  14.6 18.6 %all-to-all-start = ((s32[128,1,128]{2,1,0:T(1,128)}), s32[128,1,128]{2,1,0:T(1,128)S(1)}, u32[]{:S(2)}, u32[]{:S(2)}) async-start(s32[128,1,128]{2,1,0:T(1,128)} %broadcast_in_dim.9), calls=%async_computation | async-start | bytes 131072 | tf_op jit(solution)/shard_map/all_to_all | solution.py:592
  33.2 0.6 copy-start.5
  39.5 15.7 %all-to-all-start.1 = ((f32[128,4,128]{2,1,0:T(4,128)}), f32[128,4,128]{2,1,0:T(4,128)S(1)}, u32[]{:S(2)}, u32[]{:S(2)}) async-start(f32[128,4,128]{2,1,0:T(4,128)} %bitcast.24), calls=%async_computation.1 | async-start | bytes 524288 | tf_op jit(solution)/shard_map/all_to_all | solution.py:572
  44.2 50.4 %copy-start = (bf16[80,8,8,128]{3,2,1,0:T(8,128)(2,1)}, bf16[80,8,8,128]{3,2,1,0:T(8,128)(2,1)S(1)}, u32[]{:S(2)}) copy-start(bf16[80,8,8,128]{3,2,1,0:T(8,128)(2,1)S(1)} %collective-permute-done.1.refs_3_.refs_2_) | copy-start | bytes 3932164
  44.2 50.4 %collective-permute-start.7 = (bf16[80,8,8,128]{3,2,1,0:T(8,128)(2,1)S(1)}, bf16[80,8,8,128]{3,2,1,0:T(8,128)(2,1)}, u32[]{:S(2)}, u32[]{:S(2)}) collective-permute-start(bf16[80,8,8,128]{3,2,1,0:T(8,128)(2,1)S(1)} %collective-permute-done.1.refs_3_.refs_2_), channel_id=1, source_target_pairs={{0,112},{16,0},{32,16},{48,32},{64,48},{80,64},{96,80},{112,96},{1... | collective-permute-start | bytes 3932168 | tf_op jit(solution)/shard_map/ppermute | solution.py:548
  46.1 48.5 %copy-start.1 = (bf16[80,8,8,128]{3,2,1,0:T(8,128)(2,1)}, bf16[80,8,8,128]{3,2,1,0:T(8,128)(2,1)S(1)}, u32[]{:S(2)}) copy-start(bf16[80,8,8,128]{3,2,1,0:T(8,128)(2,1)S(1)} %collective-permute-done.refs_1_.refs_0_) | copy-start | bytes 3932164
  46.1 48.5 %collective-permute-start.6 = (bf16[80,8,8,128]{3,2,1,0:T(8,128)(2,1)S(1)}, bf16[80,8,8,128]{3,2,1,0:T(8,128)(2,1)}, u32[]{:S(2)}, u32[]{:S(2)}) collective-permute-start(bf16[80,8,8,128]{3,2,1,0:T(8,128)(2,1)S(1)} %collective-permute-done.refs_1_.refs_0_), channel_id=1, source_target_pairs={{0,16},{16,32},{32,48},{48,64},{64,80},{80,96},{96,112},{112,0},{1... | collective-permute-start | bytes 3932168 | tf_op jit(solution)/shard_map/ppermute | solution.py:548
  55.3 0.7 copy-start.4
  58.8 4.3 %collective-permute-start.13 = (f32[10,8,128]{2,1,0:T(8,128)}, f32[10,8,128]{2,1,0:T(8,128)S(1)}, u32[]{:S(2)}, u32[]{:S(2)}) collective-permute-start(f32[10,8,128]{2,1,0:T(8,128)} %columns.2.refs_2_.refs_12_), channel_id=1, source_target_pairs={{0,96},{16,112},{32,0},{48,16},{64,32},{80,48},{96,64},{112,80},{1... | collective-permute-start | bytes 122888 | tf_op jit(solution)/shard_map/ppermute | solution.py:548
  59.7 3.4 %collective-permute-start.12 = (f32[10,8,128]{2,1,0:T(8,128)}, f32[10,8,128]{2,1,0:T(8,128)S(1)}, u32[]{:S(2)}, u32[]{:S(2)}) collective-permute-start(f32[10,8,128]{2,1,0:T(8,128)} %columns.2.refs_2_.refs_12_), channel_id=1, source_target_pairs={{0,112},{16,0},{32,16},{48,32},{64,48},{80,64},{96,80},{112,96},{1... | collective-permute-start | bytes 122888 | tf_op jit(solution)/shard_map/ppermute | solution.py:548
  60.7 33.9 %copy-start.2 = (bf16[80,2,8,128]{3,2,1,0:T(8,128)(2,1)}, bf16[80,2,8,128]{3,2,1,0:T(8,128)(2,1)S(1)}, u32[]{:S(2)}) copy-start(bf16[80,2,8,128]{3,2,1,0:T(8,128)(2,1)S(1)} %broadcast_select_fusion.refs_7_.refs_4_) | copy-start | bytes 983044
  60.7 10.9 %collective-permute-start.5 = (bf16[80,2,8,128]{3,2,1,0:T(8,128)(2,1)S(1)}, bf16[80,2,8,128]{3,2,1,0:T(8,128)(2,1)S(1)}, u32[]{:S(2)}, u32[]{:S(2)}) collective-permute-start(bf16[80,2,8,128]{3,2,1,0:T(8,128)(2,1)S(1)} %broadcast_select_fusion.refs_7_.refs_4_), channel_id=1, source_target_pairs={{0,112},{16,0},{32,16},{48,32},{64,48},{80,64},{96,80},{112,96},{1... | collective-permute-start | bytes 983048 | tf_op jit(solution)/shard_map/ppermute | solution.py:548
  63.1 14.0 %copy-start.9 = (f32[10,8,128]{2,1,0:T(8,128)}, f32[10,8,128]{2,1,0:T(8,128)S(1)}, u32[]{:S(2)}) copy-start(f32[10,8,128]{2,1,0:T(8,128)S(1)} %collective-permute-done.13.refs_4_.refs_14_) | copy-start | bytes 122884
  63.1 8.8 %collective-permute-start.4 = (bf16[80,2,8,128]{3,2,1,0:T(8,128)(2,1)S(1)}, bf16[80,2,8,128]{3,2,1,0:T(8,128)(2,1)}, u32[]{:S(2)}, u32[]{:S(2)}) collective-permute-start(bf16[80,2,8,128]{3,2,1,0:T(8,128)(2,1)S(1)} %broadcast_select_fusion.refs_7_.refs_4_), channel_id=1, source_target_pairs={{0,16},{16,32},{32,48},{48,64},{64,80},{80,96},{96,112},{112,0},{1... | collective-permute-start | bytes 983048 | tf_op jit(solution)/shard_map/ppermute | solution.py:548
  63.1 14.0 %copy-start.10 = (f32[10,8,128]{2,1,0:T(8,128)}, f32[10,8,128]{2,1,0:T(8,128)S(1)}, u32[]{:S(2)}) copy-start(f32[10,8,128]{2,1,0:T(8,128)S(1)} %collective-permute-done.12.refs_3_.refs_13_) | copy-start | bytes 122884
  63.2 8.1 %collective-permute-start.11 = (f32[10,8,128]{2,1,0:T(8,128)}, f32[10,8,128]{2,1,0:T(8,128)S(1)}, u32[]{:S(2)}, u32[]{:S(2)}) collective-permute-start(f32[10,8,128]{2,1,0:T(8,128)} %columns.2.refs_2_.refs_12_), channel_id=1, source_target_pairs={{0,16},{16,32},{32,48},{48,64},{64,80},{80,96},{96,112},{112,0},{1... | collective-permute-start | bytes 122888 | tf_op jit(solution)/shard_map/ppermute | solution.py:548
  71.3 5.8 %copy-start.11 = (f32[10,8,128]{2,1,0:T(8,128)}, f32[10,8,128]{2,1,0:T(8,128)S(1)}, u32[]{:S(2)}) copy-start(f32[10,8,128]{2,1,0:T(8,128)S(1)} %collective-permute-done.11.refs_1_.refs_11_) | copy-start | bytes 122884
  71.3 5.8 %collective-permute-start.10 = (f32[10,8,128]{2,1,0:T(8,128)}, f32[10,8,128]{2,1,0:T(8,128)S(1)}, u32[]{:S(2)}, u32[]{:S(2)}) collective-permute-start(f32[10,8,128]{2,1,0:T(8,128)} %columns.2.refs_2_.refs_12_), channel_id=1, source_target_pairs={{0,32},{16,48},{32,64},{48,80},{64,96},{80,112},{96,0},{112,16},{1... | collective-permute-start | bytes 122888 | tf_op jit(solution)/shard_map/ppermute | solution.py:548
  71.6 23.0 %copy-start.3 = (bf16[80,2,8,128]{3,2,1,0:T(8,128)(2,1)}, bf16[80,2,8,128]{3,2,1,0:T(8,128)(2,1)S(1)}, u32[]{:S(2)}) copy-start(bf16[80,2,8,128]{3,2,1,0:T(8,128)(2,1)S(1)} %collective-permute-done.5.refs_8_.refs_5_) | copy-start | bytes 983044
  71.6 23.0 %collective-permute-start.9 = (bf16[80,2,8,128]{3,2,1,0:T(8,128)(2,1)S(1)}, bf16[80,2,8,128]{3,2,1,0:T(8,128)(2,1)}, u32[]{:S(2)}, u32[]{:S(2)}) collective-permute-start(bf16[80,2,8,128]{3,2,1,0:T(8,128)(2,1)S(1)} %collective-permute-done.5.refs_8_.refs_5_), channel_id=1, source_target_pairs={{0,112},{16,0},{32,16},{48,32},{64,48},{80,64},{96,80},{112,96},{1... | collective-permute-start | bytes 983048 | tf_op jit(solution)/shard_map/ppermute | solution.py:548
  71.9 22.7 %collective-permute-start.8 = (bf16[80,2,8,128]{3,2,1,0:T(8,128)(2,1)}, bf16[80,2,8,128]{3,2,1,0:T(8,128)(2,1)}, u32[]{:S(2)}, u32[]{:S(2)}) collective-permute-start(bf16[80,2,8,128]{3,2,1,0:T(8,128)(2,1)} %collective-permute-done.4.refs_6_.refs_3_), channel_id=1, source_target_pairs={{0,16},{16,32},{32,48},{48,64},{64,80},{80,96},{96,112},{112,0},{1... | collective-permute-start | bytes 983048 | tf_op jit(solution)/shard_map/ppermute | solution.py:548
  77.1 0.6 copy-start.12
  79.2 7.6 %collective-permute-start.15 = (f32[5,2,8,128]{3,2,1,0:T(8,128)}, f32[5,2,8,128]{3,2,1,0:T(8,128)S(1)}, u32[]{:S(2)}, u32[]{:S(2)}) collective-permute-start(f32[5,2,8,128]{3,2,1,0:T(8,128)} %edges.2), channel_id=1, source_target_pairs={{0,15},{1,0},{2,1},{3,2},{4,3},{5,4},{6,5},{7,6},{8,7},{9,8},{10,9... | collective-permute-start | bytes 122888 | tf_op jit(solution)/shard_map/ppermute | solution.py:548
  86.8 7.8 %copy-start.13 = (f32[5,2,8,128]{3,2,1,0:T(8,128)}, f32[5,2,8,128]{3,2,1,0:T(8,128)S(1)}, u32[]{:S(2)}) copy-start(f32[5,2,8,128]{3,2,1,0:T(8,128)S(1)} %collective-permute-done.15.refs_16_) | copy-start | bytes 122884
  86.8 7.7 %collective-permute-start.14 = (f32[5,2,8,128]{3,2,1,0:T(8,128)}, f32[5,2,8,128]{3,2,1,0:T(8,128)S(1)}, u32[]{:S(2)}, u32[]{:S(2)}) collective-permute-start(f32[5,2,8,128]{3,2,1,0:T(8,128)} %edges.2), channel_id=1, source_target_pairs={{0,1},{1,2},{2,3},{3,4},{4,5},{5,6},{6,7},{7,8},{8,9},{9,10},{10,1... | collective-permute-start | bytes 122888 | tf_op jit(solution)/shard_map/ppermute | solution.py:548
  87.5 7.1 %copy-start.6 = (f32[5,8,128]{2,1,0:T(8,128)}, f32[5,8,128]{2,1,0:T(8,128)S(1)}, u32[]{:S(2)}) copy-start(f32[5,8,128]{2,1,0:T(8,128)S(1)} %constant_dynamic-update-slice_fusion.refs_19_.coef_ref.refs_13_) | copy-start | bytes 61444
  94.6 0.6 copy-start.14
  155.9 2.6 %collective-permute-start.17 = (f32[10,8,128]{2,1,0:T(8,128)}, f32[10,8,128]{2,1,0:T(8,128)S(1)}, u32[]{:S(2)}, u32[]{:S(2)}) collective-permute-start(f32[10,8,128]{2,1,0:T(8,128)} %columns.3.refs_1_.refs_7_), channel_id=1, source_target_pairs={{0,112},{16,0},{32,16},{48,32},{64,48},{80,64},{96,80},{112,96},{1... | collective-permute-start | bytes 122888 | tf_op jit(solution)/shard_map/ppermute | solution.py:548
  156.5 4.8 %collective-permute-start.16 = (f32[10,8,128]{2,1,0:T(8,128)}, f32[10,8,128]{2,1,0:T(8,128)S(1)}, u32[]{:S(2)}, u32[]{:S(2)}) collective-permute-start(f32[10,8,128]{2,1,0:T(8,128)} %columns.3.refs_1_.refs_7_), channel_id=1, source_target_pairs={{0,16},{16,32},{32,48},{48,64},{64,80},{80,96},{96,112},{112,0},{1... | collective-permute-start | bytes 122888 | tf_op jit(solution)/shard_map/ppermute | solution.py:548
  158.5 2.9 %copy-start.7 = (f32[10,8,128]{2,1,0:T(8,128)}, f32[10,8,128]{2,1,0:T(8,128)S(1)}, u32[]{:S(2)}) copy-start(f32[10,8,128]{2,1,0:T(8,128)S(1)} %collective-permute-done.17.refs_2_.refs_8_) | copy-start | bytes 122884
  161.3 0.6 copy-start.8
  163.4 4.0 %collective-permute-start.19 = (f32[3,2,8,128]{3,2,1,0:T(8,128)}, f32[3,2,8,128]{3,2,1,0:T(8,128)S(1)}, u32[]{:S(2)}, u32[]{:S(2)}) collective-permute-start(f32[3,2,8,128]{3,2,1,0:T(8,128)} %edges.3), channel_id=1, source_target_pairs={{0,15},{1,0},{2,1},{3,2},{4,3},{5,4},{6,5},{7,6},{8,7},{9,8},{10,9... | collective-permute-start | bytes 73736 | tf_op jit(solution)/shard_map/ppermute | solution.py:548
  164.6 7.4 %collective-permute-start.18 = (f32[3,2,8,128]{3,2,1,0:T(8,128)}, f32[3,2,8,128]{3,2,1,0:T(8,128)S(1)}, u32[]{:S(2)}, u32[]{:S(2)}) collective-permute-start(f32[3,2,8,128]{3,2,1,0:T(8,128)} %edges.3), channel_id=1, source_target_pairs={{0,1},{1,2},{2,3},{3,4},{4,5},{5,6},{6,7},{7,8},{8,9},{9,10},{10,1... | collective-permute-start | bytes 73736 | tf_op jit(solution)/shard_map/ppermute | solution.py:548
  167.4 4.5 %copy-start.16 = (f32[3,2,8,128]{3,2,1,0:T(8,128)}, f32[3,2,8,128]{3,2,1,0:T(8,128)S(1)}, u32[]{:S(2)}) copy-start(f32[3,2,8,128]{3,2,1,0:T(8,128)S(1)} %collective-permute-done.19.refs_10_) | copy-start | bytes 73732
  172.0 0.6 copy-start.17
where the time goes:
time: 184 us; the launch traced here: 183 us
  Pallas kernels  55.6 us (30%)
  waiting for transfers between devices  47.2 us (26%)
  starting transfers between devices  36.3 us (20%)
  blocking collectives  33 us (18%)
  local copies, waits for them, and re-layouts  6.76 us (4%)
  between operations  2.95 us (2%)
    all_to_all x2, blocking collectives, route(): lax.all_to_all(buffer, ('lat', 'lon'), split_axis=0, concat_axis=0, tiled...  33 us
    ppermute x20, waiting for transfers between devices, shift(): lax.ppermute(value, axis, [(i, (i + step) % count) for i in range(count)])  30.5 us
    ppermute x20, starting transfers between devices, shift(): lax.ppermute(value, axis, [(i, (i + step) % count) for i in range(count)])  22.6 us
    pallas_call x1, Pallas kernels, middle(): pl.pallas_call(middle_kernel, grid=(LEV,), out_shape=jax.ShapeDtypeStruct...  11.5 us
    pallas_call x1, Pallas kernels, second(): pl.pallas_call(second_kernel, out_shape=(jax.ShapeDtypeStruct((BUF, LANES...  10.8 us
    pallas_call x1, Pallas kernels, final(): pl.pallas_call(final_kernel, grid=(LEV,), out_shape=(jax.ShapeDtypeStruct...  10.1 us
    all_to_all x1, starting transfers between devices, per_device(): lax.all_to_all(counts, ('lat', 'lon'), split_axis=0, concat_axis=0, tiled...  9.11 us
    all_to_all x1, waiting for transfers between devices, per_device(): lax.all_to_all(counts, ('lat', 'lon'), split_axis=0, concat_axis=0, tiled...  8.9 us
  transfers between devices with their start and end apart: 22, of which 11 were waited for; matrix products, arithmetic and copies ran while one was open for 2% of the time, Pallas kernels for 9%

commit v1 on v0

--- a/solution.py
+++ b/solution.py
@@ -1,3 +1,4 @@
+import functools
 import math
 
 import jax
@@ -26,6 +27,7 @@
 TAPS = 17
 EDGE = 16
 BUF = DEV * 4
+PAIRS = DEV // 2
 
 VMEM = pltpu.VMEM
 ARB = ("arbitrary",)
@@ -33,6 +35,10 @@
 
 def whole(memory_space=VMEM):
     return pl.BlockSpec(memory_space=memory_space)
+
+
+def near(*arrays):
+    return [pltpu.with_memory_space_constraint(a, VMEM) for a in arrays]
 
 
 def split(value):
@@ -52,8 +58,27 @@
     return lax.dot_general(a, b, (((1,), (1,)), ((), ())), preferred_element_type=F32)
 
 
-def matrices_kernel(band_ref, lat_ref, lon_ref, lat_mid, lon_mid, lat_fin, lon_fin):
+def matrices_kernel(
+    band_ref, lat_ref, lon_ref, sigma_ref, step_ref, cols_ref,
+    lat_mid, lon_mid, lat_fin, lon_fin, coef_ref, cell_ref,
+):
     base = band_ref[0] * ROWS
+    cell_ref[...] = jnp.concatenate(
+        [cols_ref[pl.ds(h, PAIRS, stride=2), :] for h in range(2)], axis=1
+    )
+    ens_scale = HYBRID_ENSEMBLE / math.sqrt(MEM - 1)
+    level = iota((LEV, LANES), 0)
+    sigma = jnp.zeros((LEV, LANES), F32)
+    for l in range(LEV):
+        sigma = jnp.where(level == l, sigma_ref[l], sigma)
+    once = jnp.ones((LEV, LANES), F32)
+    step0 = once * step_ref[0]
+    step1 = once * step_ref[1]
+    coef_ref[0] = step0 * (-ens_scale * ens_scale)
+    coef_ref[1] = step0 * sigma * sigma * (-HYBRID_STATIC * HYBRID_STATIC)
+    coef_ref[2] = sigma * -HYBRID_STATIC
+    coef_ref[3] = (1.0 - step1) * step0
+    coef_ref[4] = step1
 
     def pick(index, taps):
         out = jnp.zeros(index.shape, F32)
@@ -128,7 +153,7 @@
     place(lon_fin, pick(HW - main, lon_ref), pick(HW - edge, lon_ref))
 
 
-def matrices(band, lat_taps, lon_taps):
+def matrices(band, lat_taps, lon_taps, static_sigma, step_len, cols):
     smem = whole(pltpu.SMEM)
     return pl.pallas_call(
         matrices_kernel,
@@ -137,12 +162,14 @@
             jax.ShapeDtypeStruct((4, 256, 256), BF16),
             jax.ShapeDtypeStruct((64, 192), BF16),
             jax.ShapeDtypeStruct((4, 256, 256), BF16),
+            jax.ShapeDtypeStruct((5, LEV, LANES), F32),
+            jax.ShapeDtypeStruct((PAIRS, LANES), I32),
         ),
-        in_specs=[smem] * 3,
-        out_specs=(whole(),) * 4,
+        in_specs=[smem] * 5 + [whole()],
+        out_specs=(whole(),) * 6,
         cost_estimate=pl.CostEstimate(flops=4000000, bytes_accessed=1100000, transcendentals=0),
         name="matrices",
-    )(band, lat_taps, lon_taps)
+    )(band, lat_taps, lon_taps, static_sigma, step_len, cols)
 
 
 def pack_kernel(e_ref, out_ref):
@@ -247,7 +274,7 @@
         scratch_shapes=[VMEM((BUF, 2 * LANES), F32)],
         cost_estimate=pl.CostEstimate(flops=40000000, bytes_accessed=600000, transcendentals=0),
         name="first",
-    )(count, ref, level, weight, precision, innovation)
+    )(*near(count), ref, level, weight, precision, innovation)
 
 
 def second_kernel(
@@ -263,7 +290,7 @@
     earlier = coef_ref[3, :1, :1]
     later = coef_ref[4, :1, :1]
 
-    @pl.loop(0, NOBS // CHUNK, unroll=UNROLL)
+    @pl.loop(0, NOBS // CHUNK, unroll=1)
     def _(c):
         part = pl.ds(pl.multiple_of(c * CHUNK, CHUNK), CHUNK)
         rows = [row_ref[q : q + 1, part] for q in range(4)]
@@ -298,7 +325,7 @@
         scratch_shapes=[VMEM((BUF, 2 * LANES), F32)],
         cost_estimate=pl.CostEstimate(flops=60000000, bytes_accessed=800000, transcendentals=0),
         name="second",
-    )(incoming, rows, lanes, weight, precision, innovation, coefs)
+    )(*near(incoming, rows, lanes), weight, precision, innovation, *near(coefs))
 
 
 def swap_quadrants(tile):
@@ -308,7 +335,6 @@
     return jnp.where(sub == lane, tile, moved)
 
 
-PAIRS = DEV // 2
 GROUP = 4
 
 
@@ -357,7 +383,7 @@
         scratch_shapes=[VMEM((64, LANES), F32)],
         cost_estimate=pl.CostEstimate(flops=20000000, bytes_accessed=400000, transcendentals=0),
         name="columns",
-    )(buffer, cells)
+    )(*near(buffer, cells))
 
 
 def slots_kernel(increment_ref, cell_ref, out_ref):
@@ -390,52 +416,97 @@
         out_specs=whole(),
         cost_estimate=pl.CostEstimate(flops=20000000, bytes_accessed=400000, transcendentals=0),
         name="slots",
-    )(increment, cells)
-
-
-def row_pass(e_refs, fields, lat_ref, stack, out_ref, lane0):
-    per = MEM // stack
-    wide = 2
-    lat = lat_ref[...]
-
-    def column_of(tiles):
-        value = jnp.concatenate(tiles, axis=0)
-        high = value.astype(BF16)
-        low = (value - high.astype(F32)).astype(BF16)
-        return jnp.concatenate([high, low], axis=0)
-
-    def store(row, value):
-        high = value.astype(BF16)
-        out_ref[0, row : row + 16, lane0 : lane0 + LANES] = high
-        low = (value - high.astype(F32)).astype(BF16)
-        out_ref[1, row : row + 16, lane0 : lane0 + LANES] = low
-
-    def block(value, s, n):
-        tile = value[16 * s : 16 * s + 16, n * LANES : (n + 1) * LANES]
-        return tile[:8] + tile[8:]
-
-    for c in range(0, per, wide):
+    )(*near(increment, cells))
+
+
+STEP = 16
+
+
+def column_of(tiles):
+    value = jnp.concatenate(tiles, axis=0)
+    high = value.astype(BF16)
+    low = (value - high.astype(F32)).astype(BF16)
+    return jnp.concatenate([high, low], axis=0)
+
+
+def halves(value):
+    high = value.astype(BF16)
+    return high, (value - high.astype(F32)).astype(BF16)
+
+
+def block(value, s, n):
+    tile = value[16 * s : 16 * s + 16, n * LANES : (n + 1) * LANES]
+    return tile[:8] + tile[8:]
+
+
+def filter_rows(tiles_of, fields, lat, stack):
+    per = STEP // stack
+    out = [None] * STEP
+    for c in range(0, per, 2):
         parts = []
-        for n in range(c, c + wide):
+        for n in range(c, c + 2):
             tiles = []
             for s in range(stack):
-                tiles += [e[s * per + n, 0].astype(F32) * f for e, f in zip(e_refs, fields)]
+                tiles += [t * f for t, f in zip(tiles_of(s * per + n), fields)]
             parts.append(column_of(tiles))
         value = nn(lat, jnp.concatenate(parts, axis=1))
         for s in range(stack):
-            for n in range(0, wide, 2):
-                pair = jnp.concatenate([block(value, s, n), block(value, s, n + 1)], axis=0)
-                store((s * per + c + n) * 8, pair)
-
+            for n in range(2):
+                out[s * per + c + n] = block(value, s, n)
+    return halves(jnp.concatenate(out, axis=0))
+
+
+def filter_single(fields, lat, stack):
     blank = [jnp.zeros((ROWS, LANES), F32)] * (len(fields) * (stack - 1))
-    one = block(nn(lat, column_of(list(fields) + blank)), 0, 0)
-    store(MEM * 8, jnp.concatenate([one, jnp.zeros_like(one)], axis=0))
-
-
-def column_pass(in_ref, weights, start, size):
-    value = nn(in_ref[0, start : start + size, :], weights)
-    value = value + nn(in_ref[1, start : start + size, :], weights)
+    return block(nn(lat, column_of(list(fields) + blank)), 0, 0)
+
+
+def filter_columns(high, low, weights):
+    value = nn(high, weights) + nn(low, weights)
     return value[:, :LANES] + value[:, LANES:]
+
+
+def rows_kernel(count, stack, *refs):
+    e_refs = refs[:count]
+    f_refs = refs[count : 2 * count]
+    lat_ref, out_ref, static_ref = refs[2 * count :]
+    lat = lat_ref[...]
+
+    @pl.when(pl.program_id(0) == 0)
+    def _():
+        for l in range(LEV):
+            static_ref[l] = filter_single([f[l] for f in f_refs], lat, stack)
+
+    for l in range(LEV):
+        high, low = filter_rows(
+            lambda k: [e[k, l].astype(F32) for e in e_refs], [f[l] for f in f_refs], lat, stack
+        )
+        out_ref[0, l, 0] = high
+        out_ref[0, l, 1] = low
+
+
+def member_block(depth):
+    return pl.BlockSpec((STEP, depth, ROWS, LANES), lambda i: (i, 0, 0, 0))
+
+
+def pass_block():
+    return pl.BlockSpec((1, LEV, 2, STEP * ROWS, LANES), lambda i: (i, 0, 0, 0, 0))
+
+
+def filtered(members, fields, lat, stack):
+    count = len(members)
+    return pl.pallas_call(
+        functools.partial(rows_kernel, count, stack),
+        grid=(MEM // STEP,),
+        out_shape=(
+            jax.ShapeDtypeStruct((MEM // STEP, LEV, 2, STEP * ROWS, LANES), BF16),
+            jax.ShapeDtypeStruct((LEV, ROWS, LANES), F32),
+        ),
+        in_specs=[member_block(LEV)] * count + [whole()] * (count + 1),
+        out_specs=(pass_block(), whole()),
+        compiler_params=pltpu.CompilerParams(dimension_semantics=ARB),
+        cost_estimate=pl.CostEstimate(flops=400000000, bytes_accessed=9000000, transcendentals=0),
+    )(*members, *fields, lat)
 
 
 def merge_edges(left, right):
@@ -443,104 +514,98 @@
     return jnp.where(inner < EDGE, left, right)
 
 
+def columns_of_level(main, side, weights):
+    high = jnp.concatenate([main[0], side[0]], axis=1)
+    low = jnp.concatenate([main[1], side[1]], axis=1)
+    return filter_columns(high, low, weights)
+
+
+def single_of_level(main, side, weights):
+    pad = jnp.zeros((ROWS, LANES), F32)
+    main = halves(jnp.concatenate([main, pad], axis=0))
+    side = halves(jnp.concatenate([side, pad], axis=0))
+    return columns_of_level(main, side, weights)[:ROWS]
+
+
+def side_fields(left_ref, right_ref, count, g):
+    return [merge_edges(left_ref[x, g], right_ref[x, g]) for x in range(count)]
+
+
 def middle_kernel(*refs):
-    e_refs = refs[:5]
-    h_refs = refs[5:10]
-    f_refs = refs[10:15]
-    left_ref, right_ref, lat_ref, lon_ref, coef_ref, out_ref, pass_ref = refs[15:]
-    l = pl.program_id(0)
-
-    @pl.when((l & 3) == 0)
+    h_refs = refs[:5]
+    main_ref, own_ref, static_ref, left_ref, right_ref, lat_ref, lon_ref, coef_ref, out_ref = refs[5:]
+    lat = lat_ref[...]
+    fields = [side_fields(left_ref, right_ref, 5, g) for g in range(2)]
+
+    @pl.when(pl.program_id(0) == 0)
     def _():
-        g = l >> 2
-        fields = [merge_edges(left_ref[x, g], right_ref[x, g]) for x in range(5)]
-        row_pass(h_refs, fields, lat_ref, 2, pass_ref, LANES)
-
-    fields = [f_refs[x][l] for x in range(5)]
-    row_pass(e_refs, fields, lat_ref, 2, pass_ref, 0)
-    weights = lon_ref[0]
-    step = 16
-
-    total = jnp.zeros((ROWS, LANES), F32)
-    for c in range(MEM // step):
-        value = column_pass(pass_ref, weights, c * 8 * step, 8 * step)
-        for k in range(step):
-            own = e_refs[2][c * step + k, 0].astype(F32)
-            total = total + value[8 * k : 8 * k + 8] * own
-    single = column_pass(pass_ref, weights, MEM * 8, 16)[:8]
-    out_ref[0] = coef_ref[0] * total + coef_ref[1, pl.ds(l, 1), :] * single
-
-
-def level_block(count):
-    return pl.BlockSpec((count, 1, ROWS, LANES), lambda l: (0, l, 0, 0))
-
-
-def edge_block(count):
-    return pl.BlockSpec((count, 1, ROWS, LANES), lambda l: (0, l // 4, 0, 0))
-
-
-def middle(members, halos, fields, left, right, lat_mid, lon_mid, coefs):
+        sides = [filter_single(fields[g], lat, 2) for g in range(2)]
+        for l in range(LEV):
+            single = single_of_level(static_ref[l], sides[l // 4], lon_ref[l % 4])
+            out_ref[l] = coef_ref[1, l : l + 1, :] * single
+
+    sides = [
+        filter_rows(lambda k: [h[k, g].astype(F32) for h in h_refs], fields[g], lat, 2)
+        for g in range(2)
+    ]
+    for l in range(LEV):
+        value = columns_of_level((main_ref[0, l, 0], main_ref[0, l, 1]), sides[l // 4], lon_ref[l % 4])
+        total = value[:ROWS] * own_ref[0, l].astype(F32)
+        for k in range(1, STEP):
+            total = total + value[8 * k : 8 * k + 8] * own_ref[k, l].astype(F32)
+        out_ref[l] += coef_ref[0] * total
+
+
+def middle(members, halos, passed, static, left, right, lat_mid, lon_mid, coefs):
     return pl.pallas_call(
         middle_kernel,
-        grid=(LEV,),
+        grid=(MEM // STEP,),
         out_shape=jax.ShapeDtypeStruct((LEV, ROWS, LANES), F32),
-        in_specs=[level_block(MEM)] * 5
-        + [edge_block(MEM)] * 5
-        + [whole()] * 8
-        + [pl.BlockSpec((1, 256, 256), lambda l: (l % 4, 0, 0)), whole()],
-        out_specs=pl.BlockSpec((1, ROWS, LANES), lambda l: (l, 0, 0)),
-        scratch_shapes=[VMEM((2, MEM * 8 + 16, 256), BF16)],
+        in_specs=[member_block(2)] * 5 + [pass_block(), member_block(LEV)] + [whole()] * 6,
+        out_specs=whole(),
         compiler_params=pltpu.CompilerParams(dimension_semantics=ARB),
-        cost_estimate=pl.CostEstimate(flops=100000000, bytes_accessed=9000000, transcendentals=0),
+        cost_estimate=pl.CostEstimate(flops=400000000, bytes_accessed=9000000, transcendentals=0),
         name="middle",
-    )(*members, *halos, *fields, left, right, lat_mid, lon_mid, coefs)
+    )(*halos, passed, members[2], static, left, right, lat_mid, lon_mid, coefs)
 
 
 def final_kernel(*refs):
-    e_refs = refs[:3]
-    h_refs = refs[3:6]
-    f_refs = refs[6:9]
-    left_ref, right_ref, lat_ref, lon_ref, coef_ref, out_ref, static_ref, pass_ref = refs[9:]
-    l = pl.program_id(0)
-
-    @pl.when((l & 3) == 0)
+    h_refs = refs[:3]
+    main_ref, static_ref, left_ref, right_ref, lat_ref, lon_ref, coef_ref, out_ref, single_ref = refs[3:]
+    lat = lat_ref[...]
+    fields = [side_fields(left_ref, right_ref, 3, g) for g in range(2)]
+    scale = -HYBRID_ENSEMBLE / math.sqrt(MEM - 1)
+
+    @pl.when(pl.program_id(0) == 0)
     def _():
-        g = l >> 2
-        fields = [merge_edges(left_ref[x, g], right_ref[x, g]) for x in range(3)]
-        row_pass(h_refs, fields, lat_ref, 4, pass_ref, LANES)
-
-    fields = [f_refs[x][l] for x in range(3)]
-    row_pass(e_refs, fields, lat_ref, 4, pass_ref, 0)
-    weights = lon_ref[0]
-    step = 16
-    scale = -HYBRID_ENSEMBLE / math.sqrt(MEM - 1)
-
-    for c in range(MEM // step):
-        value = column_pass(pass_ref, weights, c * 8 * step, 8 * step)
-        out_ref[c * step : (c + 1) * step, 0] = (scale * value).reshape(step, ROWS, LANES)
-
-    single = column_pass(pass_ref, weights, MEM * 8, 16)[:8]
-    static_ref[0] = coef_ref[2, pl.ds(l, 1), :] * single
-
-
-def final(members, halos, fields, left, right, lat_fin, lon_fin, coefs):
+        sides = [filter_single(fields[g], lat, 4) for g in range(2)]
+        for l in range(LEV):
+            single = single_of_level(static_ref[l], sides[l // 4], lon_ref[l % 4])
+            single_ref[l] = coef_ref[2, l : l + 1, :] * single
+
+    sides = [
+        filter_rows(lambda k: [h[k, g].astype(F32) for h in h_refs], fields[g], lat, 4)
+        for g in range(2)
+    ]
+    for l in range(LEV):
+        value = columns_of_level((main_ref[0, l, 0], main_ref[0, l, 1]), sides[l // 4], lon_ref[l % 4])
+        out_ref[:, l] = (scale * value).reshape(STEP, ROWS, LANES)
+
+
+def final(halos, passed, static, left, right, lat_fin, lon_fin, coefs):
     return pl.pallas_call(
         final_kernel,
-        grid=(LEV,),
+        grid=(MEM // STEP,),
         out_shape=(
             jax.ShapeDtypeStruct((MEM, LEV, ROWS, LANES), F32),
             jax.ShapeDtypeStruct((LEV, ROWS, LANES), F32),
         ),
-        in_specs=[level_block(MEM)] * 3
-        + [edge_block(MEM)] * 3
-        + [whole()] * 6
-        + [pl.BlockSpec((1, 256, 256), lambda l: (l % 4, 0, 0)), whole()],
-        out_specs=(level_block(MEM), pl.BlockSpec((1, ROWS, LANES), lambda l: (l, 0, 0))),
-        scratch_shapes=[VMEM((2, MEM * 8 + 16, 256), BF16)],
+        in_specs=[member_block(2)] * 3 + [pass_block()] + [whole()] * 6,
+        out_specs=(member_block(LEV), whole()),
         compiler_params=pltpu.CompilerParams(dimension_semantics=ARB),
-        cost_estimate=pl.CostEstimate(flops=100000000, bytes_accessed=9000000, transcendentals=0),
+        cost_estimate=pl.CostEstimate(flops=400000000, bytes_accessed=9000000, transcendentals=0),
         name="final",
-    )(*members, *halos, *fields, left, right, lat_fin, lon_fin, coefs)
+    )(*halos, passed, static, left, right, lat_fin, lon_fin, coefs)
 
 
 def shift(value, axis, step):
@@ -563,7 +628,7 @@
         out_specs=whole(),
         cost_estimate=pl.CostEstimate(flops=100000, bytes_accessed=100000, transcendentals=0),
         name="edges",
-    )(*fields)
+    )(*near(*fields))
     return fields, shift(edges, "lon", 1), shift(edges, "lon", -1)
 
 
@@ -587,56 +652,45 @@
     innovation,
     obs_precision,
 ):
-    ens_scale = HYBRID_ENSEMBLE / math.sqrt(MEM - 1)
     counts = jnp.broadcast_to(send_count.reshape(DEV, 1, 1), (DEV, 1, LANES))
     received = lax.all_to_all(counts, ("lat", "lon"), split_axis=0, concat_axis=0, tiled=True)
     received = received.reshape(DEV, LANES)
-    cells = send_cols.reshape(PAIRS, LANES)
     level = obs_level.reshape(1, NOBS)
     ref = obs_ref.reshape(4, NOBS)
     weight = obs_weight.reshape(4, NOBS)
     innov = innovation.reshape(1, NOBS)
     precision = obs_precision.reshape(1, NOBS)
 
-    ones = jnp.ones((LEV, LANES), F32)
-    sigma = static_sigma[:, None] * ones
-    coefs = jnp.stack(
-        [
-            (-step_len[0] * ens_scale * ens_scale) * ones,
-            (-step_len[0] * HYBRID_STATIC * HYBRID_STATIC) * sigma * sigma,
-            -HYBRID_STATIC * sigma,
-            ((1.0 - step_len[1]) * step_len[0]) * ones,
-            step_len[1] * ones,
-        ]
+    band = lax.axis_index("lat").astype(I32).reshape(1)
+    lat_mid, lon_mid, lat_fin, lon_fin, coefs, cells = matrices(
+        band, lat_taps, lon_taps, static_sigma, step_len, send_cols.reshape(DEV, SLOT)
     )
-    band = lax.axis_index("lat").astype(I32).reshape(1)
-    lat_mid, lon_mid, lat_fin, lon_fin = matrices(band, lat_taps, lon_taps)
 
     north = shift(ensemble, "lat", 1)
     south = shift(ensemble, "lat", -1)
     packed = pack(ensemble)
     from_left = shift(packed, "lon", 1)
     from_right = shift(packed, "lon", -1)
+    north2 = shift(north, "lat", 1)
+    south2 = shift(south, "lat", -1)
+    members = [north2, north, ensemble, south, south2]
+
+    outgoing, rows, lanes = first(received, ref, level, weight, precision, innov)
+    outgoing, from_left, from_right = lax.optimization_barrier((outgoing, from_left, from_right))
     inner = lax.broadcasted_iota(I32, packed.shape, 3) & 31
     halo = jnp.where(inner < EDGE, from_left, from_right)
-    north2 = shift(north, "lat", 1)
-    south2 = shift(south, "lat", -1)
-    halo_n = shift(halo, "lat", 1)
-    halo_s = shift(halo, "lat", -1)
-    halo_n2 = shift(halo_n, "lat", 1)
-    halo_s2 = shift(halo_s, "lat", -1)
-    members = [north2, north, ensemble, south, south2]
-    halos = [halo_n2, halo_n, halo, halo_s, halo_s2]
-
-    outgoing, rows, lanes = first(received, ref, level, weight, precision, innov)
+    halos = [shift(halo, "lat", d) if d else halo for d in (2, 1, 0, -1, -2)]
+
     arrived = route(outgoing)
     forcing = columns(arrived, cells)
-    around = surround(forcing, 2)
-    increment = middle(members, halos, *around, lat_mid, lon_mid, coefs)
+    fields, left, right = surround(forcing, 2)
+    passed, static = filtered(members, fields, lat_mid, 2)
+    increment = middle(members, halos, passed, static, left, right, lat_mid, lon_mid, coefs)
     incoming = route(slots(increment.reshape(LEV * ROWS, LANES), cells))
     outgoing, departure = second(incoming, rows, lanes, weight, precision, innov, coefs)
-    around = surround(columns(route(outgoing), cells), 1)
-    control, static = final(members[1:4], halos[1:4], *around, lat_fin, lon_fin, coefs)
+    fields, left, right = surround(columns(route(outgoing), cells), 1)
+    passed, static = filtered(members[1:4], fields, lat_fin, 4)
+    control, static = final(halos[1:4], passed, static, left, right, lat_fin, lon_fin, coefs)
     return (control, static, departure.reshape(1, 1, -1))
 
 

time: 184 us -> 182 us (0.989)
  waiting for transfers between devices: 47.2 us -> 40.1 us
  starting transfers between devices: 36.3 us -> 43.2 us
  between operations: 2.95 us -> 0.9 us
    ppermute x20, starting transfers between devices: 22.6 us -> 34 us  [shift(): lax.ppermute(value, axis, [(i, (i + step) % count) for i in range(count)])]
    pallas_call x2 -> x4, Pallas kernels: 21.6 us -> 28.6 us  [the longest x2 14.2 us: filtered(): pl.pallas_call(functools.partial(rows_kernel, count, stack), grid=(MEM //...]
    ppermute x20, waiting for transfers between devices: 30.5 us -> 23.8 us  [shift(): lax.ppermute(value, axis, [(i, (i + step) % count) for i in range(count)])]
    all_to_all x1, starting transfers between devices: 9.11 us -> 4.52 us  [per_device(): lax.all_to_all(counts, ('lat', 'lon'), split_axis=0, concat_axis=0, tiled...]
    unnamed x47 -> x53, local copies, waits for them, and re-layouts: 4 us -> 5.98 us
    pallas_call x2, Pallas kernels: 5.64 us -> 3.73 us  [columns(): pl.pallas_call(columns_kernel, out_shape=jax.ShapeDtypeStruct((LEV + 2, R...]
  transfers between devices with their start and end apart: 22 -> 22, of which waited for: 11 -> 7; matrix products, arithmetic and copies ran while one was open for 2% -> 1% of each run, Pallas kernels for 9% -> 16%
where the time goes in v1:
time: 182 us; the launch traced here: 180 us
  Pallas kernels  56.7 us (31%)
  starting transfers between devices  43.2 us (24%)
  waiting for transfers between devices  40.1 us (22%)
  blocking collectives  31.6 us (17%)
  local copies, waits for them, and re-layouts  6.79 us (4%)
    ppermute x20, starting transfers between devices, shift(): lax.ppermute(value, axis, [(i, (i + step) % count) for i in range(count)])  34 us
    all_to_all x2, blocking collectives, route(): lax.all_to_all(buffer, ('lat', 'lon'), split_axis=0, concat_axis=0, tiled...  31.6 us
    ppermute x20, waiting for transfers between devices, shift(): lax.ppermute(value, axis, [(i, (i + step) % count) for i in range(count)])  23.8 us
    pallas_call x2, Pallas kernels, filtered(): pl.pallas_call(functools.partial(rows_kernel, count, stack), grid=(MEM //...  14.2 us
    all_to_all x1, waiting for transfers between devices, per_device(): lax.all_to_all(counts, ('lat', 'lon'), split_axis=0, concat_axis=0, tiled...  9.5 us
    pallas_call x1, Pallas kernels, second(): pl.pallas_call(second_kernel, out_shape=(jax.ShapeDtypeStruct((BUF, LANES...  9.25 us
    pallas_call x1, Pallas kernels, middle(): pl.pallas_call(middle_kernel, grid=(MEM // STEP,), out_shape=jax.ShapeDty...  7.25 us
    pallas_call x1, Pallas kernels, final(): pl.pallas_call(final_kernel, grid=(MEM // STEP,), out_shape=(jax.ShapeDty...  7.16 us
  transfers between devices with their start and end apart: 22, of which 7 were waited for; matrix products, arithmetic and copies ran while one was open for 1% of the time, Pallas kernels for 16%

profile of v1, /device:TPU:0, one launch (start us, length us, event | category | flops | bytes accessed | tf_op | source)
XLA Modules:
  0.0 180.4 jit_solution(12653789387204346766)
XLA Ops:
  0.6 0.0 collective-permute-start.4
  0.7 2.9 %collective-permute-start.5 = (bf16[80,8,8,128]{3,2,1,0:T(8,128)(2,1)}, bf16[80,8,8,128]{3,2,1,0:T(8,128)(2,1)S(1)}, u32[]{:S(2)}, u32[]{:S(2)}) collective-permute-start(bf16[80,8,8,128]{3,2,1,0:T(8,128)(2,1)} %refs_1_.1), channel_id=1, source_target_pairs={{0,112},{16,0},{32,16},{48,32},{64,48},{80,64},{96,80},{112,96},{1... | collective-permute-start | bytes 3932168 | tf_op jit(solution)/shard_map/ppermute | solution.py:613
  3.6 15.5 %collective-permute-done.4.refs_1_.refs_0_ = bf16[80,8,8,128]{3,2,1,0:T(8,128)(2,1)S(1)} collective-permute-done((bf16[80,8,8,128]{3,2,1,0:T(8,128)(2,1)}, bf16[80,8,8,128]{3,2,1,0:T(8,128)(2,1)S(1)}, u32[]{:S(2)}, u32[]{:S(2)}) %collective-permute-start.4) | collective-permute-done | bytes 1310752 | tf_op jit(solution)/shard_map/ppermute | solution.py:613
  19.1 2.9 %collective-permute-start.9 = (bf16[80,8,8,128]{3,2,1,0:T(8,128)(2,1)S(1)}, bf16[80,8,8,128]{3,2,1,0:T(8,128)(2,1)}, u32[]{:S(2)}, u32[]{:S(2)}) collective-permute-start(bf16[80,8,8,128]{3,2,1,0:T(8,128)(2,1)S(1)} %collective-permute-done.5.refs_3_.refs_2_), channel_id=1, source_target_pairs={{0,112},{16,0},{32,16},{48,32},{64,48},{80,64},{96,80},{112,96},{1... | collective-permute-start | bytes 3932168 | tf_op jit(solution)/shard_map/ppermute | solution.py:613
  22.1 4.2 %pack.1 = bf16[80,2,8,128]{3,2,1,0:T(8,128)(2,1)} custom-call(bf16[80,8,8,128]{3,2,1,0:T(8,128)(2,1)} %refs_1_.1), custom_call_target="tpu_custom_call" | custom-call | flops 4000000 | bytes 1600000 | tf_op jit(solution)/shard_map/pack/pallas_call | solution.py:194
  26.3 2.0 %collective-permute-start = (bf16[80,2,8,128]{3,2,1,0:T(8,128)(2,1)}, bf16[80,2,8,128]{3,2,1,0:T(8,128)(2,1)S(1)}, u32[]{:S(2)}, u32[]{:S(2)}) collective-permute-start(bf16[80,2,8,128]{3,2,1,0:T(8,128)(2,1)} %pack.1), channel_id=1, source_target_pairs={{0,1},{1,2},{2,3},{3,4},{4,5},{5,6},{6,7},{7,8},{8,9},{9,10},{10,1... | collective-permute-start | bytes 983048 | tf_op jit(solution)/shard_map/ppermute | solution.py:613
  28.3 4.6 %collective-permute-start.1 = (bf16[80,2,8,128]{3,2,1,0:T(8,128)(2,1)}, bf16[80,2,8,128]{3,2,1,0:T(8,128)(2,1)S(1)}, u32[]{:S(2)}, u32[]{:S(2)}) collective-permute-start(bf16[80,2,8,128]{3,2,1,0:T(8,128)(2,1)} %pack.1), channel_id=1, source_target_pairs={{0,15},{1,0},{2,1},{3,2},{4,3},{5,4},{6,5},{7,6},{8,7},{9,8},{10,9... | collective-permute-start | bytes 983048 | tf_op jit(solution)/shard_map/ppermute | solution.py:613
  32.9 0.8 broadcast_in_dim.8
  33.7 4.5 %all-to-all-start = ((s32[128,1,128]{2,1,0:T(1,128)}), s32[128,1,128]{2,1,0:T(1,128)S(1)}, u32[]{:S(2)}, u32[]{:S(2)}) async-start(s32[128,1,128]{2,1,0:T(1,128)} %broadcast_in_dim.8), calls=%async_computation | async-start | bytes 131072 | tf_op jit(solution)/shard_map/all_to_all | solution.py:656
  38.3 9.5 %all-to-all-done = s32[128,1,128]{2,1,0:T(1,128)S(1)} async-done(((s32[128,1,128]{2,1,0:T(1,128)}), s32[128,1,128]{2,1,0:T(1,128)S(1)}, u32[]{:S(2)}, u32[]{:S(2)}) %all-to-all-start) | async-done | bytes 65568 | tf_op jit(solution)/shard_map/all_to_all | solution.py:656
  47.8 5.7 %first.1 = (f32[512,128]{1,0:T(8,128)}, f32[4,2048]{1,0:T(4,128)}, f32[4,2048]{1,0:T(4,128)}) custom-call(s32[128,128]{1,0:T(8,128)S(1)} %bitcast.20, s32[4,2048]{1,0:T(4,128)} %bitcast.28, s32[1,2048]{1,0:T(1,128)} %bitcast.33, f32[4,2048]{1,0:T(4,128)} %bitcast.26, f32[1,2048]{1,0:T(1,128)} %bitcast.29, f32[1,2048]{1,0:T(1,128)} %bitcast.31), custom_call_target="tpu_custom_call" | custom-call | flops 40000000 | bytes 600000 | tf_op jit(solution)/shard_map/first/pallas_call | solution.py:265
  53.4 0.0 collective-permute-done
  53.5 0.0 copy-start.18
  53.5 0.7 copy-done.17
  54.2 0.1 copy-done.18
  54.3 4.6 %all-to-all-start.1 = ((f32[128,4,128]{2,1,0:T(4,128)}), f32[128,4,128]{2,1,0:T(4,128)S(1)}, u32[]{:S(2)}, u32[]{:S(2)}) async-start(f32[128,4,128]{2,1,0:T(4,128)} %bitcast.23), calls=%async_computation.1 | async-start | bytes 524288 | tf_op jit(solution)/shard_map/all_to_all | solution.py:637
  58.9 1.1 broadcast_select_fusion.refs_2_.refs_1_
  60.0 0.0 collective-permute-start.2
  60.1 0.7 copy.16
  60.8 2.2 %matrices.1 = (bf16[32,160]{1,0:T(8,128)(2,1)}, bf16[4,256,256]{2,1,0:T(8,128)(2,1)}, bf16[64,192]{1,0:T(8,128)(2,1)}, bf16[4,256,256]{2,1,0:T(8,128)(2,1)}, f32[5,8,128]{2,1,0:T(8,128)}, /*index=5*/s32[64,128]{1,0:T(8,128)}) custom-call(s32[1]{0:T(128)} %bitcast.9.band_ref, f32[17]{0:T(128)} %lat_ref.1, f32[17]{0:T(128)} %lon_ref.1, f32[8]{0:T(128)} %sigma_ref.1, ...), custom_call_target="tpu_custom_call" | custom-call | flops 4000000 | bytes 1100000 | tf_op jit(solution)/shard_map/matrices/pallas_call | solution.py:158
  63.0 6.8 %all-to-all-done.1 = f32[128,4,128]{2,1,0:T(4,128)S(1)} async-done(((f32[128,4,128]{2,1,0:T(4,128)}), f32[128,4,128]{2,1,0:T(4,128)S(1)}, u32[]{:S(2)}, u32[]{:S(2)}) %all-to-all-start.1) | async-done | bytes 262176 | tf_op jit(solution)/shard_map/all_to_all | solution.py:637
  69.7 0.8 copy-done.2
  70.5 1.9 %columns.2.refs_7_.refs_2_ = f32[10,8,128]{2,1,0:T(8,128)} custom-call(f32[512,128]{1,0:T(8,128)S(1)} %bitcast.17, s32[64,128]{1,0:T(8,128)S(1)} %copy-done.2), custom_call_target="tpu_custom_call" | custom-call | flops 20000000 | bytes 400000 | tf_op jit(solution)/shard_map/columns/pallas_call | solution.py:378
  72.4 0.6 collective-permute-start.10
  73.0 5.2 %collective-permute-done.10.refs_5_.refs_0_ = f32[10,8,128]{2,1,0:T(8,128)S(1)} collective-permute-done((f32[10,8,128]{2,1,0:T(8,128)}, f32[10,8,128]{2,1,0:T(8,128)S(1)}, u32[]{:S(2)}, u32[]{:S(2)}) %collective-permute-start.10) | collective-permute-done | bytes 40992 | tf_op jit(solution)/shard_map/ppermute | solution.py:613
  78.2 0.0 collective-permute-start.12
  78.2 0.0 collective-permute-done.11.refs_6_.refs_1_
  78.2 1.0 collective-permute-start.13
  79.2 1.1 collective-permute-done.12.refs_8_.refs_3_
  80.3 3.0 %collective-permute-start.3 = (bf16[80,2,8,128]{3,2,1,0:T(8,128)(2,1)S(1)}, bf16[80,2,8,128]{3,2,1,0:T(8,128)(2,1)}, u32[]{:S(2)}, u32[]{:S(2)}) collective-permute-start(bf16[80,2,8,128]{3,2,1,0:T(8,128)(2,1)S(1)} %broadcast_select_fusion.refs_2_.refs_1_), channel_id=1, source_target_pairs={{0,112},{16,0},{32,16},{48,32},{64,48},{80,64},{96,80},{112,96},{1... | collective-permute-start | bytes 983048 | tf_op jit(solution)/shard_map/ppermute | solution.py:613
  83.3 0.0 collective-permute-done.13.refs_9_.refs_4_
  83.3 0.0 collective-permute-start.6
  83.3 3.2 %collective-permute-start.7 = (bf16[80,2,8,128]{3,2,1,0:T(8,128)(2,1)S(1)}, bf16[80,2,8,128]{3,2,1,0:T(8,128)(2,1)}, u32[]{:S(2)}, u32[]{:S(2)}) collective-permute-start(bf16[80,2,8,128]{3,2,1,0:T(8,128)(2,1)S(1)} %broadcast_select_fusion.refs_2_.refs_1_), channel_id=1, source_target_pairs={{0,96},{16,112},{32,0},{48,16},{64,32},{80,48},{96,64},{112,80},{1... | collective-permute-start | bytes 983048 | tf_op jit(solution)/shard_map/ppermute | solution.py:613
  86.6 0.8 copy-done.1
  87.3 0.6 edges.2
  88.0 0.0 collective-permute-done.8.refs_0_
  88.0 0.8 collective-permute-start.14
  88.8 4.5 %collective-permute-start.15 = (f32[5,2,8,128]{3,2,1,0:T(8,128)}, f32[5,2,8,128]{3,2,1,0:T(8,128)S(1)}, u32[]{:S(2)}, u32[]{:S(2)}) collective-permute-start(f32[5,2,8,128]{3,2,1,0:T(8,128)} %edges.2), channel_id=1, source_target_pairs={{0,15},{1,0},{2,1},{3,2},{4,3},{5,4},{6,5},{7,6},{8,7},{9,8},{10,9... | collective-permute-start | bytes 122888 | tf_op jit(solution)/shard_map/ppermute | solution.py:613
  93.3 7.8 %shard_map.139 = (bf16[5,8,2,128,128]{4,3,2,1,0:T(8,128)(2,1)}, f32[8,8,128]{2,1,0:T(8,128)}) custom-call(bf16[80,8,8,128]{3,2,1,0:T(8,128)(2,1)} %collective-permute-done.8.refs_0_, bf16[80,8,8,128]{3,2,1,0:T(8,128)(2,1)} %copy-done.14, bf16[80,8,8,128]{3,2,1,0:T(8,128)(2,1)} %refs_1_.1, bf16[80,8,8,128]{3,2,1,0:T(8,128)(2,1)} %copy-done.15, ...), custom_call_target="tpu_custom_call" | custom-call | flops 400000000 | bytes 9000000 | tf_op jit(solution)/shard_map/pallas_call | solution.py:498
  101.1 0.0 collective-permute-done.3.refs_3_.refs_2_
  101.1 0.0 collective-permute-done.6.refs_0_
  101.2 0.0 collective-permute-done.14.refs_8_
  101.2 0.0 collective-permute-done.15.refs_9_
  101.2 0.7 copy-done.19
  101.9 0.0 copy-done.20
  101.9 0.0 copy-done.21
  101.9 7.3 %middle.1 = f32[8,8,128]{2,1,0:T(8,128)} custom-call(bf16[80,2,8,128]{3,2,1,0:T(8,128)(2,1)} %copy-done.19, bf16[80,2,8,128]{3,2,1,0:T(8,128)(2,1)} %collective-permute-done.2.refs_1_.refs_0_, bf16[80,2,8,128]{3,2,1,0:T(8,128)(2,1)} %copy-done.16, bf16[80,2,8,128]{3,2,1,0:T(8,128)(2,1)} %collective-permute-done.3.refs_3_.refs_2_, ...), custom_call_target="tpu_custom_call" | custom-call | flops 400000000 | bytes 9000000 | tf_op jit(solution)/shard_map/middle/pallas_call | solution.py:560
  109.2 0.8 copy-done.11
  110.0 1.8 %slots.1 = f32[512,128]{1,0:T(8,128)} custom-call(f32[64,128]{1,0:T(8,128)S(1)} %bitcast.21, s32[64,128]{1,0:T(8,128)S(1)} %copy-done.2), custom_call_target="tpu_custom_call" | custom-call | flops 20000000 | bytes 400000 | tf_op jit(solution)/shard_map/slots/pallas_call | solution.py:412
  111.8 15.7 %all_to_all.20 = f32[128,4,128]{2,1,0:T(4,128)S(1)} all-to-all(f32[128,4,128]{2,1,0:T(4,128)} %bitcast.22), channel_id=1, replica_groups=mesh['lat'=8,'lon'=16] {'lat','lon'}, dimensions={0} | all-to-all | bytes 524288 | tf_op jit(solution)/shard_map/all_to_all | solution.py:637
  127.5 9.3 %second.1 = (f32[512,128]{1,0:T(8,128)}, f32[1,2048]{1,0:T(1,128)}) custom-call(f32[512,128]{1,0:T(8,128)S(1)} %bitcast.18, f32[4,2048]{1,0:T(4,128)S(1)} %copy-done.12, f32[4,2048]{1,0:T(4,128)S(1)} %copy-done.13, f32[4,2048]{1,0:T(4,128)} %bitcast.27, f32[1,2048]{1,0:T(1,128)} %bitcast.30, f32[1,2048]{1,0:T(1,128)} %bitcast.32, f32[5,8,128]{2,1,0:T(8,128)S(1)} %copy-done.4), custom_call_target="tpu_custom_call" | custom-call | flops 60000000 | bytes 800000 | tf_op jit(solution)/shard_map/second/pallas_call | solution.py:317
  136.7 15.9 %all_to_all.21 = f32[128,4,128]{2,1,0:T(4,128)S(1)} all-to-all(f32[128,4,128]{2,1,0:T(4,128)} %bitcast.24), channel_id=1, replica_groups=mesh['lat'=8,'lon'=16] {'lat','lon'}, dimensions={0} | all-to-all | bytes 524288 | tf_op jit(solution)/shard_map/all_to_all | solution.py:637
  152.6 1.9 %columns.3.refs_4_.refs_1_ = f32[10,8,128]{2,1,0:T(8,128)} custom-call(f32[512,128]{1,0:T(8,128)S(1)} %bitcast.19, s32[64,128]{1,0:T(8,128)S(1)} %copy-done.3), custom_call_target="tpu_custom_call" | custom-call | flops 20000000 | bytes 400000 | tf_op jit(solution)/shard_map/columns/pallas_call | solution.py:378
  154.5 3.0 %collective-permute-start.17 = (f32[10,8,128]{2,1,0:T(8,128)}, f32[10,8,128]{2,1,0:T(8,128)S(1)}, u32[]{:S(2)}, u32[]{:S(2)}) collective-permute-start(f32[10,8,128]{2,1,0:T(8,128)} %columns.3.refs_4_.refs_1_), channel_id=1, source_target_pairs={{0,112},{16,0},{32,16},{48,32},{64,48},{80,64},{96,80},{112,96},{1... | collective-permute-start | bytes 122888 | tf_op jit(solution)/shard_map/ppermute | solution.py:613
  157.4 1.9 %collective-permute-done.16.refs_3_.refs_0_ = f32[10,8,128]{2,1,0:T(8,128)S(1)} collective-permute-done((f32[10,8,128]{2,1,0:T(8,128)}, f32[10,8,128]{2,1,0:T(8,128)S(1)}, u32[]{:S(2)}, u32[]{:S(2)}) %collective-permute-start.16) | collective-permute-done | bytes 40992 | tf_op jit(solution)/shard_map/ppermute | solution.py:613
  159.3 0.1 collective-permute-done.17.refs_5_.refs_2_
  159.4 0.8 copy-done
  160.2 0.6 edges.3
  160.8 0.8 collective-permute-start.18
  161.7 4.5 %collective-permute-start.19 = (f32[3,2,8,128]{3,2,1,0:T(8,128)}, f32[3,2,8,128]{3,2,1,0:T(8,128)S(1)}, u32[]{:S(2)}, u32[]{:S(2)}) collective-permute-start(f32[3,2,8,128]{3,2,1,0:T(8,128)} %edges.3), channel_id=1, source_target_pairs={{0,15},{1,0},{2,1},{3,2},{4,3},{5,4},{6,5},{7,6},{8,7},{9,8},{10,9... | collective-permute-start | bytes 73736 | tf_op jit(solution)/shard_map/ppermute | solution.py:613
  166.2 6.4 %shard_map.140 = (bf16[5,8,2,128,128]{4,3,2,1,0:T(8,128)(2,1)}, f32[8,8,128]{2,1,0:T(8,128)}) custom-call(bf16[80,8,8,128]{3,2,1,0:T(8,128)(2,1)} %copy-done.14, bf16[80,8,8,128]{3,2,1,0:T(8,128)(2,1)} %refs_1_.1, bf16[80,8,8,128]{3,2,1,0:T(8,128)(2,1)} %copy-done.15, f32[10,8,128]{2,1,0:T(8,128)} %copy-done.5, f32[10,8,128]{2,1,0:T(8,128)} %columns.3.refs_4_.refs_1_, ...), custom_call_target="tpu_custom_call" | custom-call | flops 400000000 | bytes 9000000 | tf_op jit(solution)/shard_map/pallas_call | solution.py:498
  172.6 0.6 copy-done.23
  173.2 0.0 copy-done.24
  173.2 7.2 %final.1 = (f32[80,8,8,128]{3,2,1,0:T(8,128)}, f32[8,8,128]{2,1,0:T(8,128)}) custom-call(bf16[80,2,8,128]{3,2,1,0:T(8,128)(2,1)} %collective-permute-done.2.refs_1_.refs_0_, bf16[80,2,8,128]{3,2,1,0:T(8,128)(2,1)} %copy-done.16, bf16[80,2,8,128]{3,2,1,0:T(8,128)(2,1)} %collective-permute-done.3.refs_3_.refs_2_, ...), custom_call_target="tpu_custom_call" | custom-call | flops 400000000 | bytes 9000000 | tf_op jit(solution)/shard_map/final/pallas_call | solution.py:596
  (51 shorter events, 0.1 us)
Async XLA Ops:
  0.6 32.3 %copy-start.25 = (s32[1,1,128]{2,1,0:T(1,128)S(1)}, s32[1,1,128]{2,1,0:T(1,128)}, u32[]{:S(2)}) copy-start(s32[1,1,128]{2,1,0:T(1,128)} %param.18) | copy-start | bytes 1540
  0.6 18.5 %collective-permute-start.4 = (bf16[80,8,8,128]{3,2,1,0:T(8,128)(2,1)}, bf16[80,8,8,128]{3,2,1,0:T(8,128)(2,1)S(1)}, u32[]{:S(2)}, u32[]{:S(2)}) collective-permute-start(bf16[80,8,8,128]{3,2,1,0:T(8,128)(2,1)} %refs_1_.1), channel_id=1, source_target_pairs={{0,16},{16,32},{32,48},{48,64},{64,80},{80,96},{96,112},{112,0},{1... | collective-permute-start | bytes 3932168 | tf_op jit(solution)/shard_map/ppermute | solution.py:613
  0.7 18.4 %collective-permute-start.5 = (bf16[80,8,8,128]{3,2,1,0:T(8,128)(2,1)}, bf16[80,8,8,128]{3,2,1,0:T(8,128)(2,1)S(1)}, u32[]{:S(2)}, u32[]{:S(2)}) collective-permute-start(bf16[80,8,8,128]{3,2,1,0:T(8,128)(2,1)} %refs_1_.1), channel_id=1, source_target_pairs={{0,112},{16,0},{32,16},{48,32},{64,48},{80,64},{96,80},{112,96},{1... | collective-permute-start | bytes 3932168 | tf_op jit(solution)/shard_map/ppermute | solution.py:613
  19.1 40.9 %copy-start.14 = (bf16[80,8,8,128]{3,2,1,0:T(8,128)(2,1)}, bf16[80,8,8,128]{3,2,1,0:T(8,128)(2,1)S(1)}, u32[]{:S(2)}) copy-start(bf16[80,8,8,128]{3,2,1,0:T(8,128)(2,1)S(1)} %collective-permute-done.4.refs_1_.refs_0_) | copy-start | bytes 3932164
  19.1 68.9 %collective-permute-start.8 = (bf16[80,8,8,128]{3,2,1,0:T(8,128)(2,1)S(1)}, bf16[80,8,8,128]{3,2,1,0:T(8,128)(2,1)}, u32[]{:S(2)}, u32[]{:S(2)}) collective-permute-start(bf16[80,8,8,128]{3,2,1,0:T(8,128)(2,1)S(1)} %collective-permute-done.4.refs_1_.refs_0_), channel_id=1, source_target_pairs={{0,16},{16,32},{32,48},{48,64},{64,80},{80,96},{96,112},{112,0},{1... | collective-permute-start | bytes 3932168 | tf_op jit(solution)/shard_map/ppermute | solution.py:613
  19.1 40.9 %copy-start.15 = (bf16[80,8,8,128]{3,2,1,0:T(8,128)(2,1)}, bf16[80,8,8,128]{3,2,1,0:T(8,128)(2,1)S(1)}, u32[]{:S(2)}) copy-start(bf16[80,8,8,128]{3,2,1,0:T(8,128)(2,1)S(1)} %collective-permute-done.5.refs_3_.refs_2_) | copy-start | bytes 3932164
  19.1 69.7 %collective-permute-start.9 = (bf16[80,8,8,128]{3,2,1,0:T(8,128)(2,1)S(1)}, bf16[80,8,8,128]{3,2,1,0:T(8,128)(2,1)}, u32[]{:S(2)}, u32[]{:S(2)}) collective-permute-start(bf16[80,8,8,128]{3,2,1,0:T(8,128)(2,1)S(1)} %collective-permute-done.5.refs_3_.refs_2_), channel_id=1, source_target_pairs={{0,112},{16,0},{32,16},{48,32},{64,48},{80,64},{96,80},{112,96},{1... | collective-permute-start | bytes 3932168 | tf_op jit(solution)/shard_map/ppermute | solution.py:613
  26.3 33.7 %copy-start.22 = (s32[1,1,128,64]{2,3,1,0:T(8,128)S(1)}, s32[1,1,128,64]{2,3,1,0:T(8,128)}, u32[]{:S(2)}) copy-start(s32[1,1,128,64]{2,3,1,0:T(8,128)} %param.17) | copy-start | bytes 98308
  26.3 27.1 %collective-permute-start = (bf16[80,2,8,128]{3,2,1,0:T(8,128)(2,1)}, bf16[80,2,8,128]{3,2,1,0:T(8,128)(2,1)S(1)}, u32[]{:S(2)}, u32[]{:S(2)}) collective-permute-start(bf16[80,2,8,128]{3,2,1,0:T(8,128)(2,1)} %pack.1), channel_id=1, source_target_pairs={{0,1},{1,2},{2,3},{3,4},{4,5},{5,6},{6,7},{7,8},{8,9},{9,10},{10,1... | collective-permute-start | bytes 983048 | tf_op jit(solution)/shard_map/ppermute | solution.py:613
  28.3 25.1 %collective-permute-start.1 = (bf16[80,2,8,128]{3,2,1,0:T(8,128)(2,1)}, bf16[80,2,8,128]{3,2,1,0:T(8,128)(2,1)S(1)}, u32[]{:S(2)}, u32[]{:S(2)}) collective-permute-start(bf16[80,2,8,128]{3,2,1,0:T(8,128)(2,1)} %pack.1), channel_id=1, source_target_pairs={{0,15},{1,0},{2,1},{3,2},{4,3},{5,4},{6,5},{7,6},{8,7},{9,8},{10,9... | collective-permute-start | bytes 983048 | tf_op jit(solution)/shard_map/ppermute | solution.py:613
  33.7 14.0 %all-to-all-start = ((s32[128,1,128]{2,1,0:T(1,128)}), s32[128,1,128]{2,1,0:T(1,128)S(1)}, u32[]{:S(2)}, u32[]{:S(2)}) async-start(s32[128,1,128]{2,1,0:T(1,128)} %broadcast_in_dim.8), calls=%async_computation | async-start | bytes 131072 | tf_op jit(solution)/shard_map/all_to_all | solution.py:656
  53.4 0.7 copy-start.17
  53.5 0.8 copy-start.18
  54.3 15.5 %all-to-all-start.1 = ((f32[128,4,128]{2,1,0:T(4,128)}), f32[128,4,128]{2,1,0:T(4,128)S(1)}, u32[]{:S(2)}, u32[]{:S(2)}) async-start(f32[128,4,128]{2,1,0:T(4,128)} %bitcast.23), calls=%async_computation.1 | async-start | bytes 524288 | tf_op jit(solution)/shard_map/all_to_all | solution.py:637
  60.0 41.1 %copy-start.16 = (bf16[80,2,8,128]{3,2,1,0:T(8,128)(2,1)}, bf16[80,2,8,128]{3,2,1,0:T(8,128)(2,1)S(1)}, u32[]{:S(2)}) copy-start(bf16[80,2,8,128]{3,2,1,0:T(8,128)(2,1)S(1)} %broadcast_select_fusion.refs_2_.refs_1_) | copy-start | bytes 983044
  60.0 23.3 %collective-permute-start.2 = (bf16[80,2,8,128]{3,2,1,0:T(8,128)(2,1)S(1)}, bf16[80,2,8,128]{3,2,1,0:T(8,128)(2,1)}, u32[]{:S(2)}, u32[]{:S(2)}) collective-permute-start(bf16[80,2,8,128]{3,2,1,0:T(8,128)(2,1)S(1)} %broadcast_select_fusion.refs_2_.refs_1_), channel_id=1, source_target_pairs={{0,16},{16,32},{32,48},{48,64},{64,80},{80,96},{96,112},{112,0},{1... | collective-permute-start | bytes 983048 | tf_op jit(solution)/shard_map/ppermute | solution.py:613
  69.7 0.8 copy-start.2
  72.4 5.8 %collective-permute-start.10 = (f32[10,8,128]{2,1,0:T(8,128)}, f32[10,8,128]{2,1,0:T(8,128)S(1)}, u32[]{:S(2)}, u32[]{:S(2)}) collective-permute-start(f32[10,8,128]{2,1,0:T(8,128)} %columns.2.refs_7_.refs_2_), channel_id=1, source_target_pairs={{0,32},{16,48},{32,64},{48,80},{64,96},{80,112},{96,0},{112,16},{1... | collective-permute-start | bytes 122888 | tf_op jit(solution)/shard_map/ppermute | solution.py:613
  73.0 5.3 %collective-permute-start.11 = (f32[10,8,128]{2,1,0:T(8,128)}, f32[10,8,128]{2,1,0:T(8,128)S(1)}, u32[]{:S(2)}, u32[]{:S(2)}) collective-permute-start(f32[10,8,128]{2,1,0:T(8,128)} %columns.2.refs_7_.refs_2_), channel_id=1, source_target_pairs={{0,16},{16,32},{32,48},{48,64},{64,80},{80,96},{96,112},{112,0},{1... | collective-permute-start | bytes 122888 | tf_op jit(solution)/shard_map/ppermute | solution.py:613
  78.2 15.1 %copy-start.7 = (f32[10,8,128]{2,1,0:T(8,128)}, f32[10,8,128]{2,1,0:T(8,128)S(1)}, u32[]{:S(2)}) copy-start(f32[10,8,128]{2,1,0:T(8,128)S(1)} %collective-permute-done.10.refs_5_.refs_0_) | copy-start | bytes 122884
  78.2 2.1 %collective-permute-start.12 = (f32[10,8,128]{2,1,0:T(8,128)}, f32[10,8,128]{2,1,0:T(8,128)S(1)}, u32[]{:S(2)}, u32[]{:S(2)}) collective-permute-start(f32[10,8,128]{2,1,0:T(8,128)} %columns.2.refs_7_.refs_2_), channel_id=1, source_target_pairs={{0,112},{16,0},{32,16},{48,32},{64,48},{80,64},{96,80},{112,96},{1... | collective-permute-start | bytes 122888 | tf_op jit(solution)/shard_map/ppermute | solution.py:613
  78.2 15.1 %copy-start.8 = (f32[10,8,128]{2,1,0:T(8,128)}, f32[10,8,128]{2,1,0:T(8,128)S(1)}, u32[]{:S(2)}) copy-start(f32[10,8,128]{2,1,0:T(8,128)S(1)} %collective-permute-done.11.refs_6_.refs_1_) | copy-start | bytes 122884
  78.2 5.1 %collective-permute-start.13 = (f32[10,8,128]{2,1,0:T(8,128)}, f32[10,8,128]{2,1,0:T(8,128)S(1)}, u32[]{:S(2)}, u32[]{:S(2)}) collective-permute-start(f32[10,8,128]{2,1,0:T(8,128)} %columns.2.refs_7_.refs_2_), channel_id=1, source_target_pairs={{0,96},{16,112},{32,0},{48,16},{64,32},{80,48},{96,64},{112,80},{1... | collective-permute-start | bytes 122888 | tf_op jit(solution)/shard_map/ppermute | solution.py:613
  80.3 13.0 %copy-start.9 = (f32[10,8,128]{2,1,0:T(8,128)}, f32[10,8,128]{2,1,0:T(8,128)S(1)}, u32[]{:S(2)}) copy-start(f32[10,8,128]{2,1,0:T(8,128)S(1)} %collective-permute-done.12.refs_8_.refs_3_) | copy-start | bytes 122884
  80.3 20.8 %collective-permute-start.3 = (bf16[80,2,8,128]{3,2,1,0:T(8,128)(2,1)S(1)}, bf16[80,2,8,128]{3,2,1,0:T(8,128)(2,1)}, u32[]{:S(2)}, u32[]{:S(2)}) collective-permute-start(bf16[80,2,8,128]{3,2,1,0:T(8,128)(2,1)S(1)} %broadcast_select_fusion.refs_2_.refs_1_), channel_id=1, source_target_pairs={{0,112},{16,0},{32,16},{48,32},{64,48},{80,64},{96,80},{112,96},{1... | collective-permute-start | bytes 983048 | tf_op jit(solution)/shard_map/ppermute | solution.py:613
  83.3 10.0 %copy-start.10 = (f32[10,8,128]{2,1,0:T(8,128)}, f32[10,8,128]{2,1,0:T(8,128)S(1)}, u32[]{:S(2)}) copy-start(f32[10,8,128]{2,1,0:T(8,128)S(1)} %collective-permute-done.13.refs_9_.refs_4_) | copy-start | bytes 122884
  83.3 17.8 %collective-permute-start.6 = (bf16[80,2,8,128]{3,2,1,0:T(8,128)(2,1)S(1)}, bf16[80,2,8,128]{3,2,1,0:T(8,128)(2,1)S(1)}, u32[]{:S(2)}, u32[]{:S(2)}) collective-permute-start(bf16[80,2,8,128]{3,2,1,0:T(8,128)(2,1)S(1)} %broadcast_select_fusion.refs_2_.refs_1_), channel_id=1, source_target_pairs={{0,32},{16,48},{32,64},{48,80},{64,96},{80,112},{96,0},{112,16},{1... | collective-permute-start | bytes 983048 | tf_op jit(solution)/shard_map/ppermute | solution.py:613
  83.3 17.8 %collective-permute-start.7 = (bf16[80,2,8,128]{3,2,1,0:T(8,128)(2,1)S(1)}, bf16[80,2,8,128]{3,2,1,0:T(8,128)(2,1)}, u32[]{:S(2)}, u32[]{:S(2)}) collective-permute-start(bf16[80,2,8,128]{3,2,1,0:T(8,128)(2,1)S(1)} %broadcast_select_fusion.refs_2_.refs_1_), channel_id=1, source_target_pairs={{0,96},{16,112},{32,0},{48,16},{64,32},{80,48},{96,64},{112,80},{1... | collective-permute-start | bytes 983048 | tf_op jit(solution)/shard_map/ppermute | solution.py:613
  86.6 0.8 copy-start.1
  88.0 13.2 %collective-permute-start.14 = (f32[5,2,8,128]{3,2,1,0:T(8,128)}, f32[5,2,8,128]{3,2,1,0:T(8,128)S(1)}, u32[]{:S(2)}, u32[]{:S(2)}) collective-permute-start(f32[5,2,8,128]{3,2,1,0:T(8,128)} %edges.2), channel_id=1, source_target_pairs={{0,1},{1,2},{2,3},{3,4},{4,5},{5,6},{6,7},{7,8},{8,9},{9,10},{10,1... | collective-permute-start | bytes 122888 | tf_op jit(solution)/shard_map/ppermute | solution.py:613
  88.8 12.4 %collective-permute-start.15 = (f32[5,2,8,128]{3,2,1,0:T(8,128)}, f32[5,2,8,128]{3,2,1,0:T(8,128)S(1)}, u32[]{:S(2)}, u32[]{:S(2)}) collective-permute-start(f32[5,2,8,128]{3,2,1,0:T(8,128)} %edges.2), channel_id=1, source_target_pairs={{0,15},{1,0},{2,1},{3,2},{4,3},{5,4},{6,5},{7,6},{8,7},{9,8},{10,9... | collective-permute-start | bytes 122888 | tf_op jit(solution)/shard_map/ppermute | solution.py:613
  101.1 0.7 copy-start.19
  101.2 0.7 copy-start.20
  101.2 0.7 copy-start.21
  101.9 25.6 %copy-start.4 = (f32[5,8,128]{2,1,0:T(8,128)S(1)}, f32[5,8,128]{2,1,0:T(8,128)}, u32[]{:S(2)}) copy-start(f32[5,8,128]{2,1,0:T(8,128)} %get-tuple-element.32.refs_12_.coef_ref.refs_9_) | copy-start | bytes 61444
  101.9 25.6 %copy-start.12 = (f32[4,2048]{1,0:T(4,128)S(1)}, f32[4,2048]{1,0:T(4,128)}, u32[]{:S(2)}) copy-start(f32[4,2048]{1,0:T(4,128)} %get-tuple-element.33.row_ref) | copy-start | bytes 98308
  101.9 25.6 %copy-start.13 = (f32[4,2048]{1,0:T(4,128)S(1)}, f32[4,2048]{1,0:T(4,128)}, u32[]{:S(2)}) copy-start(f32[4,2048]{1,0:T(4,128)} %get-tuple-element.34.lane_ref) | copy-start | bytes 98308
  109.2 43.4 %copy-start.3 = (s32[64,128]{1,0:T(8,128)S(1)}, s32[64,128]{1,0:T(8,128)}, u32[]{:S(2)}) copy-start(s32[64,128]{1,0:T(8,128)} %get-tuple-element.27.cell_ref) | copy-start | bytes 98308
  109.2 0.8 copy-start.11
  154.5 4.8 %collective-permute-start.16 = (f32[10,8,128]{2,1,0:T(8,128)}, f32[10,8,128]{2,1,0:T(8,128)S(1)}, u32[]{:S(2)}, u32[]{:S(2)}) collective-permute-start(f32[10,8,128]{2,1,0:T(8,128)} %columns.3.refs_4_.refs_1_), channel_id=1, source_target_pairs={{0,16},{16,32},{32,48},{48,64},{64,80},{80,96},{96,112},{112,0},{1... | collective-permute-start | bytes 122888 | tf_op jit(solution)/shard_map/ppermute | solution.py:613
  154.5 4.9 %collective-permute-start.17 = (f32[10,8,128]{2,1,0:T(8,128)}, f32[10,8,128]{2,1,0:T(8,128)S(1)}, u32[]{:S(2)}, u32[]{:S(2)}) collective-permute-start(f32[10,8,128]{2,1,0:T(8,128)} %columns.3.refs_4_.refs_1_), channel_id=1, source_target_pairs={{0,112},{16,0},{32,16},{48,32},{64,48},{80,64},{96,80},{112,96},{1... | collective-permute-start | bytes 122888 | tf_op jit(solution)/shard_map/ppermute | solution.py:613
  159.3 6.8 %copy-start.5 = (f32[10,8,128]{2,1,0:T(8,128)}, f32[10,8,128]{2,1,0:T(8,128)S(1)}, u32[]{:S(2)}) copy-start(f32[10,8,128]{2,1,0:T(8,128)S(1)} %collective-permute-done.16.refs_3_.refs_0_) | copy-start | bytes 122884
  159.4 0.8 copy-start
  160.2 6.0 %copy-start.6 = (f32[10,8,128]{2,1,0:T(8,128)}, f32[10,8,128]{2,1,0:T(8,128)S(1)}, u32[]{:S(2)}) copy-start(f32[10,8,128]{2,1,0:T(8,128)S(1)} %collective-permute-done.17.refs_5_.refs_2_) | copy-start | bytes 122884
  160.8 11.7 %collective-permute-start.18 = (f32[3,2,8,128]{3,2,1,0:T(8,128)}, f32[3,2,8,128]{3,2,1,0:T(8,128)S(1)}, u32[]{:S(2)}, u32[]{:S(2)}) collective-permute-start(f32[3,2,8,128]{3,2,1,0:T(8,128)} %edges.3), channel_id=1, source_target_pairs={{0,1},{1,2},{2,3},{3,4},{4,5},{5,6},{6,7},{7,8},{8,9},{9,10},{10,1... | collective-permute-start | bytes 73736 | tf_op jit(solution)/shard_map/ppermute | solution.py:613
  161.7 10.9 %collective-permute-start.19 = (f32[3,2,8,128]{3,2,1,0:T(8,128)}, f32[3,2,8,128]{3,2,1,0:T(8,128)S(1)}, u32[]{:S(2)}, u32[]{:S(2)}) collective-permute-start(f32[3,2,8,128]{3,2,1,0:T(8,128)} %edges.3), channel_id=1, source_target_pairs={{0,15},{1,0},{2,1},{3,2},{4,3},{5,4},{6,5},{7,6},{8,7},{9,8},{10,9... | collective-permute-start | bytes 73736 | tf_op jit(solution)/shard_map/ppermute | solution.py:613
  172.6 0.6 copy-start.23
  172.6 0.6 copy-start.24

commit v2 on v1

--- a/solution.py
+++ b/solution.py
@@ -31,14 +31,19 @@
 
 VMEM = pltpu.VMEM
 ARB = ("arbitrary",)
+LIMIT = 20 * 2**20
 
 
 def whole(memory_space=VMEM):
     return pl.BlockSpec(memory_space=memory_space)
 
 
+def placed(space, *arrays):
+    return [pltpu.with_memory_space_constraint(a, space) for a in arrays]
+
+
 def near(*arrays):
-    return [pltpu.with_memory_space_constraint(a, VMEM) for a in arrays]
+    return placed(VMEM, *arrays)
 
 
 def split(value):
@@ -158,18 +163,19 @@
     return pl.pallas_call(
         matrices_kernel,
         out_shape=(
-            jax.ShapeDtypeStruct((32, 160), BF16),
-            jax.ShapeDtypeStruct((4, 256, 256), BF16),
-            jax.ShapeDtypeStruct((64, 192), BF16),
-            jax.ShapeDtypeStruct((4, 256, 256), BF16),
-            jax.ShapeDtypeStruct((5, LEV, LANES), F32),
-            jax.ShapeDtypeStruct((PAIRS, LANES), I32),
+            VMEM((32, 160), BF16),
+            VMEM((4, 256, 256), BF16),
+            VMEM((64, 192), BF16),
+            VMEM((4, 256, 256), BF16),
+            VMEM((5, LEV, LANES), F32),
+            VMEM((PAIRS, LANES), I32),
         ),
         in_specs=[smem] * 5 + [whole()],
         out_specs=(whole(),) * 6,
+        compiler_params=pltpu.CompilerParams(vmem_limit_bytes=LIMIT),
         cost_estimate=pl.CostEstimate(flops=4000000, bytes_accessed=1100000, transcendentals=0),
         name="matrices",
-    )(band, lat_taps, lon_taps, static_sigma, step_len, cols)
+    )(band, *placed(pltpu.HBM, lat_taps, lon_taps, static_sigma, step_len), cols)
 
 
 def pack_kernel(e_ref, out_ref):
@@ -178,13 +184,19 @@
     inner = col & 31
     source = jnp.where(inner < EDGE, inner + LANES - EDGE, inner - EDGE)
     count = e_ref.shape[0]
+    chooses = []
+    for v in range(4):
+        choose = jnp.logical_and(row == source, (col >> 5) == v)
+        chooses.append(jnp.where(choose, 1.0, 0.0).astype(BF16))
+    choose = [jnp.concatenate(chooses[2 * h : 2 * h + 2], axis=0) for h in range(2)]
     for g in range(2):
         total = None
-        for v in range(4):
-            choose = jnp.logical_and(row == source, (col >> 5) == v)
-            choose = jnp.where(choose, 1.0, 0.0).astype(BF16)
-            tile = e_ref[:, 4 * g + v].astype(F32).reshape(count * ROWS, LANES).astype(BF16)
-            part = nn(tile, choose)
+        for h in range(2):
+            tiles = [
+                e_ref[:, 4 * g + 2 * h + v].astype(F32).reshape(count * ROWS, LANES).astype(BF16)
+                for v in range(2)
+            ]
+            part = nn(jnp.concatenate(tiles, axis=1), choose[h])
             total = part if total is None else total + part
         out_ref[:, g] = total.reshape(count, ROWS, LANES).astype(BF16)
 
@@ -197,7 +209,7 @@
         out_shape=jax.ShapeDtypeStruct((MEM, 2, ROWS, LANES), BF16),
         in_specs=[pl.BlockSpec((step, LEV, ROWS, LANES), lambda i: (i, 0, 0, 0))],
         out_specs=pl.BlockSpec((step, 2, ROWS, LANES), lambda i: (i, 0, 0, 0)),
-        compiler_params=pltpu.CompilerParams(dimension_semantics=ARB),
+        compiler_params=pltpu.CompilerParams(dimension_semantics=ARB, vmem_limit_bytes=LIMIT),
         cost_estimate=pl.CostEstimate(flops=4000000, bytes_accessed=1600000, transcendentals=0),
         name="pack",
     )(ensemble)
@@ -266,12 +278,13 @@
         first_kernel,
         out_shape=(
             jax.ShapeDtypeStruct((BUF, LANES), F32),
-            jax.ShapeDtypeStruct((4, NOBS), F32),
-            jax.ShapeDtypeStruct((4, NOBS), F32),
+            VMEM((4, NOBS), F32),
+            VMEM((4, NOBS), F32),
         ),
         in_specs=[whole()] * 6,
         out_specs=(whole(),) * 3,
         scratch_shapes=[VMEM((BUF, 2 * LANES), F32)],
+        compiler_params=pltpu.CompilerParams(vmem_limit_bytes=LIMIT),
         cost_estimate=pl.CostEstimate(flops=40000000, bytes_accessed=600000, transcendentals=0),
         name="first",
     )(*near(count), ref, level, weight, precision, innovation)
@@ -323,9 +336,10 @@
         in_specs=[whole()] * 7,
         out_specs=(whole(),) * 2,
         scratch_shapes=[VMEM((BUF, 2 * LANES), F32)],
+        compiler_params=pltpu.CompilerParams(vmem_limit_bytes=LIMIT),
         cost_estimate=pl.CostEstimate(flops=60000000, bytes_accessed=800000, transcendentals=0),
         name="second",
-    )(*near(incoming, rows, lanes), weight, precision, innovation, *near(coefs))
+    )(*near(incoming), rows, lanes, weight, precision, innovation, coefs)
 
 
 def swap_quadrants(tile):
@@ -377,13 +391,14 @@
 def columns(buffer, cells):
     return pl.pallas_call(
         columns_kernel,
-        out_shape=jax.ShapeDtypeStruct((LEV + 2, ROWS, LANES), F32),
+        out_shape=VMEM((LEV + 2, ROWS, LANES), F32),
         in_specs=[whole()] * 2,
         out_specs=whole(),
         scratch_shapes=[VMEM((64, LANES), F32)],
+        compiler_params=pltpu.CompilerParams(vmem_limit_bytes=LIMIT),
         cost_estimate=pl.CostEstimate(flops=20000000, bytes_accessed=400000, transcendentals=0),
         name="columns",
-    )(*near(buffer, cells))
+    )(*near(buffer), cells)
 
 
 def slots_kernel(increment_ref, cell_ref, out_ref):
@@ -414,9 +429,10 @@
         out_shape=jax.ShapeDtypeStruct((BUF, LANES), F32),
         in_specs=[whole()] * 2,
         out_specs=whole(),
+        compiler_params=pltpu.CompilerParams(vmem_limit_bytes=LIMIT),
         cost_estimate=pl.CostEstimate(flops=20000000, bytes_accessed=400000, transcendentals=0),
         name="slots",
-    )(*near(increment, cells))
+    )(*near(increment), cells)
 
 
 STEP = 16
@@ -471,6 +487,8 @@
     f_refs = refs[count : 2 * count]
     lat_ref, out_ref, static_ref = refs[2 * count :]
     lat = lat_ref[...]
+    step = pl.program_id(0)
+    base = step * STEP
 
     @pl.when(pl.program_id(0) == 0)
     def _():
@@ -479,18 +497,14 @@
 
     for l in range(LEV):
         high, low = filter_rows(
-            lambda k: [e[k, l].astype(F32) for e in e_refs], [f[l] for f in f_refs], lat, stack
+            lambda k: [e[base + k, l].astype(F32) for e in e_refs], [f[l] for f in f_refs], lat, stack
         )
-        out_ref[0, l, 0] = high
-        out_ref[0, l, 1] = low
+        out_ref[step, l, 0] = high
+        out_ref[step, l, 1] = low
 
 
 def member_block(depth):
     return pl.BlockSpec((STEP, depth, ROWS, LANES), lambda i: (i, 0, 0, 0))
-
-
-def pass_block():
-    return pl.BlockSpec((1, LEV, 2, STEP * ROWS, LANES), lambda i: (i, 0, 0, 0, 0))
 
 
 def filtered(members, fields, lat, stack):
@@ -499,14 +513,14 @@
         functools.partial(rows_kernel, count, stack),
         grid=(MEM // STEP,),
         out_shape=(
-            jax.ShapeDtypeStruct((MEM // STEP, LEV, 2, STEP * ROWS, LANES), BF16),
-            jax.ShapeDtypeStruct((LEV, ROWS, LANES), F32),
+            VMEM((MEM // STEP, LEV, 2, STEP * ROWS, LANES), BF16),
+            VMEM((LEV, ROWS, LANES), F32),
         ),
-        in_specs=[member_block(LEV)] * count + [whole()] * (count + 1),
-        out_specs=(pass_block(), whole()),
-        compiler_params=pltpu.CompilerParams(dimension_semantics=ARB),
+        in_specs=[whole()] * (2 * count + 1),
+        out_specs=(whole(), whole()),
+        compiler_params=pltpu.CompilerParams(dimension_semantics=ARB, vmem_limit_bytes=LIMIT),
         cost_estimate=pl.CostEstimate(flops=400000000, bytes_accessed=9000000, transcendentals=0),
-    )(*members, *fields, lat)
+    )(*near(*members, *fields), lat)
 
 
 def merge_edges(left, right):
@@ -536,6 +550,8 @@
     main_ref, own_ref, static_ref, left_ref, right_ref, lat_ref, lon_ref, coef_ref, out_ref = refs[5:]
     lat = lat_ref[...]
     fields = [side_fields(left_ref, right_ref, 5, g) for g in range(2)]
+    step = pl.program_id(0)
+    base = step * STEP
 
     @pl.when(pl.program_id(0) == 0)
     def _():
@@ -545,14 +561,14 @@
             out_ref[l] = coef_ref[1, l : l + 1, :] * single
 
     sides = [
-        filter_rows(lambda k: [h[k, g].astype(F32) for h in h_refs], fields[g], lat, 2)
+        filter_rows(lambda k: [h[base + k, g].astype(F32) for h in h_refs], fields[g], lat, 2)
         for g in range(2)
     ]
     for l in range(LEV):
-        value = columns_of_level((main_ref[0, l, 0], main_ref[0, l, 1]), sides[l // 4], lon_ref[l % 4])
-        total = value[:ROWS] * own_ref[0, l].astype(F32)
+        value = columns_of_level((main_ref[step, l, 0], main_ref[step, l, 1]), sides[l // 4], lon_ref[l % 4])
+        total = value[:ROWS] * own_ref[base, l].astype(F32)
         for k in range(1, STEP):
-            total = total + value[8 * k : 8 * k + 8] * own_ref[k, l].astype(F32)
+            total = total + value[8 * k : 8 * k + 8] * own_ref[base + k, l].astype(F32)
         out_ref[l] += coef_ref[0] * total
 
 
@@ -560,13 +576,13 @@
     return pl.pallas_call(
         middle_kernel,
         grid=(MEM // STEP,),
-        out_shape=jax.ShapeDtypeStruct((LEV, ROWS, LANES), F32),
-        in_specs=[member_block(2)] * 5 + [pass_block(), member_block(LEV)] + [whole()] * 6,
+        out_shape=VMEM((LEV, ROWS, LANES), F32),
+        in_specs=[whole()] * 13,
         out_specs=whole(),
-        compiler_params=pltpu.CompilerParams(dimension_semantics=ARB),
+        compiler_params=pltpu.CompilerParams(dimension_semantics=ARB, vmem_limit_bytes=LIMIT),
         cost_estimate=pl.CostEstimate(flops=400000000, bytes_accessed=9000000, transcendentals=0),
         name="middle",
-    )(*halos, passed, members[2], static, left, right, lat_mid, lon_mid, coefs)
+    )(*near(*halos, passed, members[2], static, left, right), lat_mid, lon_mid, coefs)
 
 
 def final_kernel(*refs):
@@ -574,6 +590,8 @@
     main_ref, static_ref, left_ref, right_ref, lat_ref, lon_ref, coef_ref, out_ref, single_ref = refs[3:]
     lat = lat_ref[...]
     fields = [side_fields(left_ref, right_ref, 3, g) for g in range(2)]
+    step = pl.program_id(0)
+    base = step * STEP
     scale = -HYBRID_ENSEMBLE / math.sqrt(MEM - 1)
 
     @pl.when(pl.program_id(0) == 0)
@@ -584,11 +602,11 @@
             single_ref[l] = coef_ref[2, l : l + 1, :] * single
 
     sides = [
-        filter_rows(lambda k: [h[k, g].astype(F32) for h in h_refs], fields[g], lat, 4)
+        filter_rows(lambda k: [h[base + k, g].astype(F32) for h in h_refs], fields[g], lat, 4)
         for g in range(2)
     ]
     for l in range(LEV):
-        value = columns_of_level((main_ref[0, l, 0], main_ref[0, l, 1]), sides[l // 4], lon_ref[l % 4])
+        value = columns_of_level((main_ref[step, l, 0], main_ref[step, l, 1]), sides[l // 4], lon_ref[l % 4])
         out_ref[:, l] = (scale * value).reshape(STEP, ROWS, LANES)
 
 
@@ -600,12 +618,12 @@
             jax.ShapeDtypeStruct((MEM, LEV, ROWS, LANES), F32),
             jax.ShapeDtypeStruct((LEV, ROWS, LANES), F32),
         ),
-        in_specs=[member_block(2)] * 3 + [pass_block()] + [whole()] * 6,
+        in_specs=[whole()] * 10,
         out_specs=(member_block(LEV), whole()),
-        compiler_params=pltpu.CompilerParams(dimension_semantics=ARB),
+        compiler_params=pltpu.CompilerParams(dimension_semantics=ARB, vmem_limit_bytes=LIMIT),
         cost_estimate=pl.CostEstimate(flops=400000000, bytes_accessed=9000000, transcendentals=0),
         name="final",
-    )(*halos, passed, static, left, right, lat_fin, lon_fin, coefs)
+    )(*near(*halos, passed, static, left, right), lat_fin, lon_fin, coefs)
 
 
 def shift(value, axis, step):
@@ -623,9 +641,10 @@
     fields = [shift(forcing, "lat", d) if d else forcing for d in bands]
     edges = pl.pallas_call(
         edges_kernel,
-        out_shape=jax.ShapeDtypeStruct((len(fields), 2, ROWS, LANES), F32),
+        out_shape=VMEM((len(fields), 2, ROWS, LANES), F32),
         in_specs=[whole()] * len(fields),
         out_specs=whole(),
+        compiler_params=pltpu.CompilerParams(vmem_limit_bytes=LIMIT),
         cost_estimate=pl.CostEstimate(flops=100000, bytes_accessed=100000, transcendentals=0),
         name="edges",
     )(*near(*fields))

time: 182 us -> 160 us (0.88)
  Pallas kernels: 56.7 us -> 37.9 us
  waiting for transfers between devices: 40.1 us -> 35.1 us
  local copies, waits for them, and re-layouts: 6.79 us -> 9.94 us
    pallas_call x6, Pallas kernels: 14.4 us -> 7.62 us  [the longest x1 3.85 us: middle(): pl.pallas_call(middle_kernel, grid=(MEM // STEP,), out_shape=VMEM((LEV, R...]
    all_to_all x1, waiting for transfers between devices: 6.78 us -> 2.68 us  [route(): lax.all_to_all(buffer, ('lat', 'lon'), split_axis=0, concat_axis=0, tiled...]
    pallas_call x2, Pallas kernels: 14.2 us -> 10.7 us  [filtered(): pl.pallas_call(functools.partial(rows_kernel, count, stack), grid=(MEM //...]
    unnamed x53 -> x55, local copies, waits for them, and re-layouts: 5.98 us -> 9.11 us
    pallas_call x1, Pallas kernels: 4.23 us -> 1.14 us  [pack(): pl.pallas_call(pack_kernel, grid=(MEM // step,), out_shape=jax.ShapeDtype...]
    pallas_call x1, Pallas kernels: 7.16 us -> 4.7 us  [final(): pl.pallas_call(final_kernel, grid=(MEM // STEP,), out_shape=(jax.ShapeDty...]
  transfers between devices with their start and end apart: 22 -> 22, of which waited for: 7 -> 6; matrix products, arithmetic and copies ran while one was open for 1% -> 2% of each run, Pallas kernels for 16% -> 12%
where the time goes in v2:
time: 160 us; the launch traced here: 159 us
  starting transfers between devices  44.4 us (28%)
  Pallas kernels  37.9 us (24%)
  waiting for transfers between devices  35.1 us (22%)
  blocking collectives  30 us (19%)
  local copies, waits for them, and re-layouts  9.94 us (6%)
    ppermute x20, starting transfers between devices, shift(): lax.ppermute(value, axis, [(i, (i + step) % count) for i in range(count)])  34.4 us
    all_to_all x2, blocking collectives, route(): lax.all_to_all(buffer, ('lat', 'lon'), split_axis=0, concat_axis=0, tiled...  30 us
    ppermute x20, waiting for transfers between devices, shift(): lax.ppermute(value, axis, [(i, (i + step) % count) for i in range(count)])  23 us
    pallas_call x2, Pallas kernels, filtered(): pl.pallas_call(functools.partial(rows_kernel, count, stack), grid=(MEM //...  10.7 us
    all_to_all x1, waiting for transfers between devices, per_device(): lax.all_to_all(counts, ('lat', 'lon'), split_axis=0, concat_axis=0, tiled...  9.42 us
    unnamed x55, local copies, waits for them, and re-layouts  9.11 us
    pallas_call x1, Pallas kernels, second(): pl.pallas_call(second_kernel, out_shape=(jax.ShapeDtypeStruct((BUF, LANES...  7.87 us
    all_to_all x1, starting transfers between devices, route(): lax.all_to_all(buffer, ('lat', 'lon'), split_axis=0, concat_axis=0, tiled...  5.35 us
  transfers between devices with their start and end apart: 22, of which 6 were waited for; matrix products, arithmetic and copies ran while one was open for 2% of the time, Pallas kernels for 12%

profile of v2, /device:TPU:0, one launch (start us, length us, event | category | flops | bytes accessed | tf_op | source)
XLA Modules:
  0.0 159.5 jit_solution(9145032345047486819)
XLA Ops:
  0.6 0.0 collective-permute-start.4
  0.7 2.9 %collective-permute-start.5 = (bf16[80,8,8,128]{3,2,1,0:T(8,128)(2,1)}, bf16[80,8,8,128]{3,2,1,0:T(8,128)(2,1)}, u32[]{:S(2)}, u32[]{:S(2)}) collective-permute-start(bf16[80,8,8,128]{3,2,1,0:T(8,128)(2,1)} %refs_1_.1), channel_id=1, source_target_pairs={{0,112},{16,0},{32,16},{48,32},{64,48},{80,64},{96,80},{112,96},{1... | collective-permute-start | bytes 3932168 | tf_op jit(solution)/shard_map/ppermute | solution.py:631
  3.6 15.5 %collective-permute-done.4.refs_1_.refs_0_ = bf16[80,8,8,128]{3,2,1,0:T(8,128)(2,1)S(1)} collective-permute-done((bf16[80,8,8,128]{3,2,1,0:T(8,128)(2,1)}, bf16[80,8,8,128]{3,2,1,0:T(8,128)(2,1)S(1)}, u32[]{:S(2)}, u32[]{:S(2)}) %collective-permute-start.4) | collective-permute-done | bytes 1310752 | tf_op jit(solution)/shard_map/ppermute | solution.py:631
  19.1 0.0 collective-permute-start.8
  19.1 0.0 collective-permute-done.5.refs_3_.refs_2_
  19.1 3.1 %collective-permute-start.9 = (bf16[80,8,8,128]{3,2,1,0:T(8,128)(2,1)}, bf16[80,8,8,128]{3,2,1,0:T(8,128)(2,1)}, u32[]{:S(2)}, u32[]{:S(2)}) collective-permute-start(bf16[80,8,8,128]{3,2,1,0:T(8,128)(2,1)} %collective-permute-done.5.refs_3_.refs_2_), channel_id=1, source_target_pairs={{0,112},{16,0},{32,16},{48,32},{64,48},{80,64},{96,80},{112,96},{1... | collective-permute-start | bytes 3932168 | tf_op jit(solution)/shard_map/ppermute | solution.py:631
  22.2 1.3 copy-done
  23.5 0.0 copy-start.23
  23.5 1.1 pack.1
  24.7 2.1 %collective-permute-start = (bf16[80,2,8,128]{3,2,1,0:T(8,128)(2,1)S(1)}, bf16[80,2,8,128]{3,2,1,0:T(8,128)(2,1)}, u32[]{:S(2)}, u32[]{:S(2)}) collective-permute-start(bf16[80,2,8,128]{3,2,1,0:T(8,128)(2,1)S(1)} %pack.1), channel_id=1, source_target_pairs={{0,1},{1,2},{2,3},{3,4},{4,5},{5,6},{6,7},{7,8},{8,9},{9,10},{10,1... | collective-permute-start | bytes 983048 | tf_op jit(solution)/shard_map/ppermute | solution.py:631
  26.8 4.7 %collective-permute-start.1 = (bf16[80,2,8,128]{3,2,1,0:T(8,128)(2,1)S(1)}, bf16[80,2,8,128]{3,2,1,0:T(8,128)(2,1)}, u32[]{:S(2)}, u32[]{:S(2)}) collective-permute-start(bf16[80,2,8,128]{3,2,1,0:T(8,128)(2,1)S(1)} %pack.1), channel_id=1, source_target_pairs={{0,15},{1,0},{2,1},{3,2},{4,3},{5,4},{6,5},{7,6},{8,7},{9,8},{10,9... | collective-permute-start | bytes 983048 | tf_op jit(solution)/shard_map/ppermute | solution.py:631
  31.4 0.8 broadcast_in_dim.8
  32.3 4.6 %all-to-all-start = ((s32[128,1,128]{2,1,0:T(1,128)}), s32[128,1,128]{2,1,0:T(1,128)S(1)}, u32[]{:S(2)}, u32[]{:S(2)}) async-start(s32[128,1,128]{2,1,0:T(1,128)} %broadcast_in_dim.8), calls=%async_computation | async-start | bytes 131072 | tf_op jit(solution)/shard_map/all_to_all | solution.py:675
  36.9 9.4 %all-to-all-done = s32[128,1,128]{2,1,0:T(1,128)S(1)} async-done(((s32[128,1,128]{2,1,0:T(1,128)}), s32[128,1,128]{2,1,0:T(1,128)S(1)}, u32[]{:S(2)}, u32[]{:S(2)}) %all-to-all-start) | async-done | bytes 65568 | tf_op jit(solution)/shard_map/all_to_all | solution.py:675
  46.3 4.8 %first.1 = (f32[512,128]{1,0:T(8,128)}, f32[4,2048]{1,0:T(4,128)S(1)}, f32[4,2048]{1,0:T(4,128)S(1)}) custom-call(s32[128,128]{1,0:T(8,128)S(1)} %bitcast.23, s32[4,2048]{1,0:T(4,128)S(1)} %bitcast.27, s32[1,2048]{1,0:T(1,128)S(1)} %bitcast.32, f32[4,2048]{1,0:T(4,128)S(1)} %bitcast.25, f32[1,2048]{1,0:T(1,128)S(1)} %bitcast.28, f32[1,2048]{1,0:T(1,128)S(1)} %bitcast.30), custom_call_target="tpu_custom_call" | custom-call | flops 40000000 | bytes 600000 | tf_op jit(solution)/shard_map/first/pallas_call | solution.py:277
  51.1 0.6 copy-done.17
  51.7 0.6 copy-done.19
  52.4 5.4 %all-to-all-start.1 = ((f32[128,4,128]{2,1,0:T(4,128)}), f32[128,4,128]{2,1,0:T(4,128)S(1)}, u32[]{:S(2)}, u32[]{:S(2)}) async-start(f32[128,4,128]{2,1,0:T(4,128)} %bitcast.7), calls=%async_computation.1 | async-start | bytes 524288 | tf_op jit(solution)/shard_map/all_to_all | solution.py:656
  57.7 1.1 broadcast_select_fusion.refs_2_.refs_1_
  58.8 0.0 collective-permute-start.2
  58.9 1.5 copy.16
  60.4 0.8 copy-done.9
  61.2 1.3 matrices.1
  62.5 0.8 copy-done.2
  63.3 0.8 copy-done.4
  64.1 0.6 copy-done.6
  64.7 0.6 copy-done.10
  65.3 0.6 copy-done.12
  65.9 2.7 %all-to-all-done.1 = f32[128,4,128]{2,1,0:T(4,128)S(1)} async-done(((f32[128,4,128]{2,1,0:T(4,128)}), f32[128,4,128]{2,1,0:T(4,128)S(1)}, u32[]{:S(2)}, u32[]{:S(2)}) %all-to-all-start.1) | async-done | bytes 262176 | tf_op jit(solution)/shard_map/all_to_all | solution.py:656
  68.6 0.8 copy-done.7
  69.3 1.2 columns.2.refs_7_.refs_2_
  70.6 0.6 collective-permute-start.10
  71.2 5.0 %collective-permute-done.10.refs_5_.refs_0_ = f32[10,8,128]{2,1,0:T(8,128)S(1)} collective-permute-done((f32[10,8,128]{2,1,0:T(8,128)S(1)}, f32[10,8,128]{2,1,0:T(8,128)S(1)}, u32[]{:S(2)}, u32[]{:S(2)}) %collective-permute-start.10) | collective-permute-done | bytes 40992 | tf_op jit(solution)/shard_map/ppermute | solution.py:631
  76.2 0.0 collective-permute-start.12
  76.2 0.0 collective-permute-done.11.refs_6_.refs_1_
  76.3 1.0 collective-permute-start.13
  77.3 0.7 collective-permute-done.12.refs_8_.refs_3_
  78.0 3.1 %collective-permute-start.3 = (bf16[80,2,8,128]{3,2,1,0:T(8,128)(2,1)S(1)}, bf16[80,2,8,128]{3,2,1,0:T(8,128)(2,1)S(1)}, u32[]{:S(2)}, u32[]{:S(2)}) collective-permute-start(bf16[80,2,8,128]{3,2,1,0:T(8,128)(2,1)S(1)} %broadcast_select_fusion.refs_2_.refs_1_), channel_id=1, source_target_pairs={{0,112},{16,0},{32,16},{48,32},{64,48},{80,64},{96,80},{112,96},{1... | collective-permute-start | bytes 983048 | tf_op jit(solution)/shard_map/ppermute | solution.py:631
  81.1 0.0 collective-permute-done.13.refs_9_.refs_4_
  81.1 0.0 collective-permute-start.6
  81.1 0.0 collective-permute-done.2.refs_1_.refs_0_
  81.2 3.2 %collective-permute-start.7 = (bf16[80,2,8,128]{3,2,1,0:T(8,128)(2,1)S(1)}, bf16[80,2,8,128]{3,2,1,0:T(8,128)(2,1)S(1)}, u32[]{:S(2)}, u32[]{:S(2)}) collective-permute-start(bf16[80,2,8,128]{3,2,1,0:T(8,128)(2,1)S(1)} %broadcast_select_fusion.refs_2_.refs_1_), channel_id=1, source_target_pairs={{0,96},{16,112},{32,0},{48,16},{64,32},{80,48},{96,64},{112,80},{1... | collective-permute-start | bytes 983048 | tf_op jit(solution)/shard_map/ppermute | solution.py:631
  84.4 0.8 collective-permute-start.14
  85.2 0.0 collective-permute-done.9.refs_4_
  85.2 4.5 %collective-permute-start.15 = (f32[5,2,8,128]{3,2,1,0:T(8,128)S(1)}, f32[5,2,8,128]{3,2,1,0:T(8,128)S(1)}, u32[]{:S(2)}, u32[]{:S(2)}) collective-permute-start(f32[5,2,8,128]{3,2,1,0:T(8,128)S(1)} %edges.2), channel_id=1, source_target_pairs={{0,15},{1,0},{2,1},{3,2},{4,3},{5,4},{6,5},{7,6},{8,7},{9,8},{10,9... | collective-permute-start | bytes 122888 | tf_op jit(solution)/shard_map/ppermute | solution.py:631
  89.7 6.4 %shard_map.139 = (bf16[5,8,2,128,128]{4,3,2,1,0:T(8,128)(2,1)S(1)}, f32[8,8,128]{2,1,0:T(8,128)S(1)}) custom-call(bf16[80,8,8,128]{3,2,1,0:T(8,128)(2,1)} %collective-permute-done.8.refs_0_, bf16[80,8,8,128]{3,2,1,0:T(8,128)(2,1)S(1)} %collective-permute-done.4.refs_1_.refs_0_, bf16[80,8,8,128]{3,2,1,0:T(8,128)(2,1)S(1)} %copy-done.1, ...), custom_call_target="tpu_custom_call" | custom-call | flops 400000000 | bytes 9000000 | tf_op jit(solution)/shard_map/pallas_call | solution.py:512
  96.2 0.0 collective-permute-done.6.refs_0_
  96.2 0.0 collective-permute-done.7.refs_4_
  96.3 0.0 copy-start.8
  96.3 0.0 copy-start.15
  96.3 0.0 copy-start.22
  96.3 0.0 copy-start.24
  96.3 3.9 %middle.1 = f32[8,8,128]{2,1,0:T(8,128)S(1)} custom-call(bf16[80,2,8,128]{3,2,1,0:T(8,128)(2,1)S(1)} %collective-permute-done.6.refs_0_, bf16[80,2,8,128]{3,2,1,0:T(8,128)(2,1)S(1)} %collective-permute-done.2.refs_1_.refs_0_, bf16[80,2,8,128]{3,2,1,0:T(8,128)(2,1)S(1)} %broadcast_select_fusion.refs_2_.refs_1_, ...), custom_call_target="tpu_custom_call" | custom-call | flops 400000000 | bytes 9000000 | tf_op jit(solution)/shard_map/middle/pallas_call | solution.py:576
  100.2 1.1 slots.1
  101.3 14.8 %all_to_all.20 = f32[128,4,128]{2,1,0:T(4,128)S(1)} all-to-all(f32[128,4,128]{2,1,0:T(4,128)S(1)} %bitcast.17), channel_id=1, replica_groups=mesh['lat'=8,'lon'=16] {'lat','lon'}, dimensions={0} | all-to-all | bytes 524288 | tf_op jit(solution)/shard_map/all_to_all | solution.py:656
  116.2 7.9 %second.1 = (f32[512,128]{1,0:T(8,128)S(1)}, f32[1,2048]{1,0:T(1,128)}) custom-call(f32[512,128]{1,0:T(8,128)S(1)} %bitcast.19, f32[4,2048]{1,0:T(4,128)S(1)} %copy-done.18, f32[4,2048]{1,0:T(4,128)S(1)} %copy-done.20, f32[4,2048]{1,0:T(4,128)S(1)} %bitcast.26, f32[1,2048]{1,0:T(1,128)S(1)} %bitcast.29, f32[1,2048]{1,0:T(1,128)S(1)} %bitcast.31, ...), custom_call_target="tpu_custom_call" | custom-call | flops 60000000 | bytes 800000 | tf_op jit(solution)/shard_map/second/pallas_call | solution.py:330
  124.1 15.2 %all_to_all.21 = f32[128,4,128]{2,1,0:T(4,128)S(1)} all-to-all(f32[128,4,128]{2,1,0:T(4,128)S(1)} %bitcast.21), channel_id=1, replica_groups=mesh['lat'=8,'lon'=16] {'lat','lon'}, dimensions={0} | all-to-all | bytes 524288 | tf_op jit(solution)/shard_map/all_to_all | solution.py:656
  139.3 1.2 columns.3.refs_4_.refs_1_
  140.5 3.0 %collective-permute-start.17 = (f32[10,8,128]{2,1,0:T(8,128)S(1)}, f32[10,8,128]{2,1,0:T(8,128)S(1)}, u32[]{:S(2)}, u32[]{:S(2)}) collective-permute-start(f32[10,8,128]{2,1,0:T(8,128)S(1)} %columns.3.refs_4_.refs_1_), channel_id=1, source_target_pairs={{0,112},{16,0},{32,16},{48,32},{64,48},{80,64},{96,80},{112,96},{1... | collective-permute-start | bytes 122888 | tf_op jit(solution)/shard_map/ppermute | solution.py:631
  143.5 1.7 %collective-permute-done.16.refs_3_.refs_0_ = f32[10,8,128]{2,1,0:T(8,128)S(1)} collective-permute-done((f32[10,8,128]{2,1,0:T(8,128)S(1)}, f32[10,8,128]{2,1,0:T(8,128)S(1)}, u32[]{:S(2)}, u32[]{:S(2)}) %collective-permute-start.16) | collective-permute-done | bytes 40992 | tf_op jit(solution)/shard_map/ppermute | solution.py:631
  145.2 0.8 collective-permute-start.18
  146.0 4.5 %collective-permute-start.19 = (f32[3,2,8,128]{3,2,1,0:T(8,128)S(1)}, f32[3,2,8,128]{3,2,1,0:T(8,128)S(1)}, u32[]{:S(2)}, u32[]{:S(2)}) collective-permute-start(f32[3,2,8,128]{3,2,1,0:T(8,128)S(1)} %edges.3), channel_id=1, source_target_pairs={{0,15},{1,0},{2,1},{3,2},{4,3},{5,4},{6,5},{7,6},{8,7},{9,8},{10,9... | collective-permute-start | bytes 73736 | tf_op jit(solution)/shard_map/ppermute | solution.py:631
  150.5 4.2 %shard_map.140 = (bf16[5,8,2,128,128]{4,3,2,1,0:T(8,128)(2,1)S(1)}, f32[8,8,128]{2,1,0:T(8,128)S(1)}) custom-call(bf16[80,8,8,128]{3,2,1,0:T(8,128)(2,1)S(1)} %collective-permute-done.4.refs_1_.refs_0_, bf16[80,8,8,128]{3,2,1,0:T(8,128)(2,1)S(1)} %copy-done.1, bf16[80,8,8,128]{3,2,1,0:T(8,128)(2,1)} %collective-permute-done.5.refs_3_.refs_2_, ...), custom_call_target="tpu_custom_call" | custom-call | flops 400000000 | bytes 9000000 | tf_op jit(solution)/shard_map/pallas_call | solution.py:512
  154.8 4.7 %final.1 = (f32[80,8,8,128]{3,2,1,0:T(8,128)}, f32[8,8,128]{2,1,0:T(8,128)}) custom-call(bf16[80,2,8,128]{3,2,1,0:T(8,128)(2,1)S(1)} %collective-permute-done.2.refs_1_.refs_0_, bf16[80,2,8,128]{3,2,1,0:T(8,128)(2,1)S(1)} %broadcast_select_fusion.refs_2_.refs_1_, bf16[80,2,8,128]{3,2,1,0:T(8,128)(2,1)S(1)} %collective-permute-done.3.refs_3_.refs_2_, ...), custom_call_target="tpu_custom_call" | custom-call | flops 400000000 | bytes 9000000 | tf_op jit(solution)/shard_map/final/pallas_call | solution.py:614
  (53 shorter events, 0.1 us)
Async XLA Ops:
  0.6 18.5 %collective-permute-start.4 = (bf16[80,8,8,128]{3,2,1,0:T(8,128)(2,1)}, bf16[80,8,8,128]{3,2,1,0:T(8,128)(2,1)S(1)}, u32[]{:S(2)}, u32[]{:S(2)}) collective-permute-start(bf16[80,8,8,128]{3,2,1,0:T(8,128)(2,1)} %refs_1_.1), channel_id=1, source_target_pairs={{0,16},{16,32},{32,48},{48,64},{64,80},{80,96},{96,112},{112,0},{1... | collective-permute-start | bytes 3932168 | tf_op jit(solution)/shard_map/ppermute | solution.py:631
  0.7 18.4 %collective-permute-start.5 = (bf16[80,8,8,128]{3,2,1,0:T(8,128)(2,1)}, bf16[80,8,8,128]{3,2,1,0:T(8,128)(2,1)}, u32[]{:S(2)}, u32[]{:S(2)}) collective-permute-start(bf16[80,8,8,128]{3,2,1,0:T(8,128)(2,1)} %refs_1_.1), channel_id=1, source_target_pairs={{0,112},{16,0},{32,16},{48,32},{64,48},{80,64},{96,80},{112,96},{1... | collective-permute-start | bytes 3932168 | tf_op jit(solution)/shard_map/ppermute | solution.py:631
  19.1 65.3 %collective-permute-start.8 = (bf16[80,8,8,128]{3,2,1,0:T(8,128)(2,1)S(1)}, bf16[80,8,8,128]{3,2,1,0:T(8,128)(2,1)}, u32[]{:S(2)}, u32[]{:S(2)}) collective-permute-start(bf16[80,8,8,128]{3,2,1,0:T(8,128)(2,1)S(1)} %collective-permute-done.4.refs_1_.refs_0_), channel_id=1, source_target_pairs={{0,16},{16,32},{32,48},{48,64},{64,80},{80,96},{96,112},{112,0},{1... | collective-permute-start | bytes 3932168 | tf_op jit(solution)/shard_map/ppermute | solution.py:631
  19.1 66.1 %collective-permute-start.9 = (bf16[80,8,8,128]{3,2,1,0:T(8,128)(2,1)}, bf16[80,8,8,128]{3,2,1,0:T(8,128)(2,1)}, u32[]{:S(2)}, u32[]{:S(2)}) collective-permute-start(bf16[80,8,8,128]{3,2,1,0:T(8,128)(2,1)} %collective-permute-done.5.refs_3_.refs_2_), channel_id=1, source_target_pairs={{0,112},{16,0},{32,16},{48,32},{64,48},{80,64},{96,80},{112,96},{1... | collective-permute-start | bytes 3932168 | tf_op jit(solution)/shard_map/ppermute | solution.py:631
  22.2 1.3 copy-start
  23.5 7.9 %copy-start.26 = (s32[1,1,128]{2,1,0:T(1,128)S(1)}, s32[1,1,128]{2,1,0:T(1,128)}, u32[]{:S(2)}) copy-start(s32[1,1,128]{2,1,0:T(1,128)} %param.18) | copy-start | bytes 1540
  23.5 22.8 %copy-start.14 = (f32[1,1,4,2048]{3,2,1,0:T(4,128)S(1)}, f32[1,1,4,2048]{3,2,1,0:T(4,128)}, u32[]{:S(2)}) copy-start(f32[1,1,4,2048]{3,2,1,0:T(4,128)} %param.21) | copy-start | bytes 98308
  23.5 22.8 %copy-start.16 = (s32[1,1,4,2048]{3,2,1,0:T(4,128)S(1)}, s32[1,1,4,2048]{3,2,1,0:T(4,128)}, u32[]{:S(2)}) copy-start(s32[1,1,4,2048]{3,2,1,0:T(4,128)} %param.19) | copy-start | bytes 98308
  23.5 22.8 %copy-start.21 = (f32[1,1,2048]{2,1,0:T(1,128)S(1)}, f32[1,1,2048]{2,1,0:T(1,128)}, u32[]{:S(2)}) copy-start(f32[1,1,2048]{2,1,0:T(1,128)} %param.23) | copy-start | bytes 24580
  23.5 22.8 %copy-start.23 = (f32[1,1,2048]{2,1,0:T(1,128)S(1)}, f32[1,1,2048]{2,1,0:T(1,128)}, u32[]{:S(2)}) copy-start(f32[1,1,2048]{2,1,0:T(1,128)} %param.22) | copy-start | bytes 24580
  23.5 22.8 %copy-start.25 = (s32[1,1,2048]{2,1,0:T(1,128)S(1)}, s32[1,1,2048]{2,1,0:T(1,128)}, u32[]{:S(2)}) copy-start(s32[1,1,2048]{2,1,0:T(1,128)} %param.20) | copy-start | bytes 24580
  24.7 27.7 %collective-permute-start = (bf16[80,2,8,128]{3,2,1,0:T(8,128)(2,1)S(1)}, bf16[80,2,8,128]{3,2,1,0:T(8,128)(2,1)}, u32[]{:S(2)}, u32[]{:S(2)}) collective-permute-start(bf16[80,2,8,128]{3,2,1,0:T(8,128)(2,1)S(1)} %pack.1), channel_id=1, source_target_pairs={{0,1},{1,2},{2,3},{3,4},{4,5},{5,6},{6,7},{7,8},{8,9},{9,10},{10,1... | collective-permute-start | bytes 983048 | tf_op jit(solution)/shard_map/ppermute | solution.py:631
  26.8 25.6 %collective-permute-start.1 = (bf16[80,2,8,128]{3,2,1,0:T(8,128)(2,1)S(1)}, bf16[80,2,8,128]{3,2,1,0:T(8,128)(2,1)}, u32[]{:S(2)}, u32[]{:S(2)}) collective-permute-start(bf16[80,2,8,128]{3,2,1,0:T(8,128)(2,1)S(1)} %pack.1), channel_id=1, source_target_pairs={{0,15},{1,0},{2,1},{3,2},{4,3},{5,4},{6,5},{7,6},{8,7},{9,8},{10,9... | collective-permute-start | bytes 983048 | tf_op jit(solution)/shard_map/ppermute | solution.py:631
  31.4 58.3 %copy-start.1 = (bf16[80,8,8,128]{3,2,1,0:T(8,128)(2,1)S(1)}, bf16[80,8,8,128]{3,2,1,0:T(8,128)(2,1)}, u32[]{:S(2)}) copy-start(bf16[80,8,8,128]{3,2,1,0:T(8,128)(2,1)} %refs_1_.1) | copy-start | bytes 3932164
  32.3 14.0 %all-to-all-start = ((s32[128,1,128]{2,1,0:T(1,128)}), s32[128,1,128]{2,1,0:T(1,128)S(1)}, u32[]{:S(2)}, u32[]{:S(2)}) async-start(s32[128,1,128]{2,1,0:T(1,128)} %broadcast_in_dim.8), calls=%async_computation | async-start | bytes 131072 | tf_op jit(solution)/shard_map/all_to_all | solution.py:675
  51.1 0.6 copy-start.17
  51.7 0.6 copy-start.19
  52.4 16.2 %all-to-all-start.1 = ((f32[128,4,128]{2,1,0:T(4,128)}), f32[128,4,128]{2,1,0:T(4,128)S(1)}, u32[]{:S(2)}, u32[]{:S(2)}) async-start(f32[128,4,128]{2,1,0:T(4,128)} %bitcast.7), calls=%async_computation.1 | async-start | bytes 524288 | tf_op jit(solution)/shard_map/all_to_all | solution.py:656
  58.8 22.3 %collective-permute-start.2 = (bf16[80,2,8,128]{3,2,1,0:T(8,128)(2,1)S(1)}, bf16[80,2,8,128]{3,2,1,0:T(8,128)(2,1)S(1)}, u32[]{:S(2)}, u32[]{:S(2)}) collective-permute-start(bf16[80,2,8,128]{3,2,1,0:T(8,128)(2,1)S(1)} %broadcast_select_fusion.refs_2_.refs_1_), channel_id=1, source_target_pairs={{0,16},{16,32},{32,48},{48,64},{64,80},{80,96},{96,112},{112,0},{1... | collective-permute-start | bytes 983048 | tf_op jit(solution)/shard_map/ppermute | solution.py:631
  60.4 0.8 copy-start.9
  62.5 0.8 copy-start.2
  63.3 0.8 copy-start.4
  64.1 0.6 copy-start.6
  64.7 0.6 copy-start.10
  65.3 0.6 copy-start.12
  68.6 0.8 copy-start.7
  70.6 5.6 %collective-permute-start.10 = (f32[10,8,128]{2,1,0:T(8,128)S(1)}, f32[10,8,128]{2,1,0:T(8,128)S(1)}, u32[]{:S(2)}, u32[]{:S(2)}) collective-permute-start(f32[10,8,128]{2,1,0:T(8,128)S(1)} %columns.2.refs_7_.refs_2_), channel_id=1, source_target_pairs={{0,32},{16,48},{32,64},{48,80},{64,96},{80,112},{96,0},{112,16},{1... | collective-permute-start | bytes 122888 | tf_op jit(solution)/shard_map/ppermute | solution.py:631
  71.2 5.0 %collective-permute-start.11 = (f32[10,8,128]{2,1,0:T(8,128)S(1)}, f32[10,8,128]{2,1,0:T(8,128)S(1)}, u32[]{:S(2)}, u32[]{:S(2)}) collective-permute-start(f32[10,8,128]{2,1,0:T(8,128)S(1)} %columns.2.refs_7_.refs_2_), channel_id=1, source_target_pairs={{0,16},{16,32},{32,48},{48,64},{64,80},{80,96},{96,112},{112,0},{1... | collective-permute-start | bytes 122888 | tf_op jit(solution)/shard_map/ppermute | solution.py:631
  76.2 1.8 %collective-permute-start.12 = (f32[10,8,128]{2,1,0:T(8,128)S(1)}, f32[10,8,128]{2,1,0:T(8,128)S(1)}, u32[]{:S(2)}, u32[]{:S(2)}) collective-permute-start(f32[10,8,128]{2,1,0:T(8,128)S(1)} %columns.2.refs_7_.refs_2_), channel_id=1, source_target_pairs={{0,112},{16,0},{32,16},{48,32},{64,48},{80,64},{96,80},{112,96},{1... | collective-permute-start | bytes 122888 | tf_op jit(solution)/shard_map/ppermute | solution.py:631
  76.3 4.9 %collective-permute-start.13 = (f32[10,8,128]{2,1,0:T(8,128)S(1)}, f32[10,8,128]{2,1,0:T(8,128)S(1)}, u32[]{:S(2)}, u32[]{:S(2)}) collective-permute-start(f32[10,8,128]{2,1,0:T(8,128)S(1)} %columns.2.refs_7_.refs_2_), channel_id=1, source_target_pairs={{0,96},{16,112},{32,0},{48,16},{64,32},{80,48},{96,64},{112,80},{1... | collective-permute-start | bytes 122888 | tf_op jit(solution)/shard_map/ppermute | solution.py:631
  78.0 18.2 %collective-permute-start.3 = (bf16[80,2,8,128]{3,2,1,0:T(8,128)(2,1)S(1)}, bf16[80,2,8,128]{3,2,1,0:T(8,128)(2,1)S(1)}, u32[]{:S(2)}, u32[]{:S(2)}) collective-permute-start(bf16[80,2,8,128]{3,2,1,0:T(8,128)(2,1)S(1)} %broadcast_select_fusion.refs_2_.refs_1_), channel_id=1, source_target_pairs={{0,112},{16,0},{32,16},{48,32},{64,48},{80,64},{96,80},{112,96},{1... | collective-permute-start | bytes 983048 | tf_op jit(solution)/shard_map/ppermute | solution.py:631
  81.1 15.1 %collective-permute-start.6 = (bf16[80,2,8,128]{3,2,1,0:T(8,128)(2,1)S(1)}, bf16[80,2,8,128]{3,2,1,0:T(8,128)(2,1)S(1)}, u32[]{:S(2)}, u32[]{:S(2)}) collective-permute-start(bf16[80,2,8,128]{3,2,1,0:T(8,128)(2,1)S(1)} %broadcast_select_fusion.refs_2_.refs_1_), channel_id=1, source_target_pairs={{0,32},{16,48},{32,64},{48,80},{64,96},{80,112},{96,0},{112,16},{1... | collective-permute-start | bytes 983048 | tf_op jit(solution)/shard_map/ppermute | solution.py:631
  81.2 15.1 %collective-permute-start.7 = (bf16[80,2,8,128]{3,2,1,0:T(8,128)(2,1)S(1)}, bf16[80,2,8,128]{3,2,1,0:T(8,128)(2,1)S(1)}, u32[]{:S(2)}, u32[]{:S(2)}) collective-permute-start(bf16[80,2,8,128]{3,2,1,0:T(8,128)(2,1)S(1)} %broadcast_select_fusion.refs_2_.refs_1_), channel_id=1, source_target_pairs={{0,96},{16,112},{32,0},{48,16},{64,32},{80,48},{96,64},{112,80},{1... | collective-permute-start | bytes 983048 | tf_op jit(solution)/shard_map/ppermute | solution.py:631
  84.4 11.8 %collective-permute-start.14 = (f32[5,2,8,128]{3,2,1,0:T(8,128)S(1)}, f32[5,2,8,128]{3,2,1,0:T(8,128)S(1)}, u32[]{:S(2)}, u32[]{:S(2)}) collective-permute-start(f32[5,2,8,128]{3,2,1,0:T(8,128)S(1)} %edges.2), channel_id=1, source_target_pairs={{0,1},{1,2},{2,3},{3,4},{4,5},{5,6},{6,7},{7,8},{8,9},{9,10},{10,1... | collective-permute-start | bytes 122888 | tf_op jit(solution)/shard_map/ppermute | solution.py:631
  85.2 11.0 %collective-permute-start.15 = (f32[5,2,8,128]{3,2,1,0:T(8,128)S(1)}, f32[5,2,8,128]{3,2,1,0:T(8,128)S(1)}, u32[]{:S(2)}, u32[]{:S(2)}) collective-permute-start(f32[5,2,8,128]{3,2,1,0:T(8,128)S(1)} %edges.2), channel_id=1, source_target_pairs={{0,15},{1,0},{2,1},{3,2},{4,3},{5,4},{6,5},{7,6},{8,7},{9,8},{10,9... | collective-permute-start | bytes 122888 | tf_op jit(solution)/shard_map/ppermute | solution.py:631
  89.7 6.5 %copy-start.5 = (bf16[4,256,256]{2,1,0:T(8,128)(2,1)S(1)}, bf16[4,256,256]{2,1,0:T(8,128)(2,1)}, u32[]{:S(2)}) copy-start(bf16[4,256,256]{2,1,0:T(8,128)(2,1)} %copy-done.4) | copy-start | bytes 1572868
  89.7 6.5 %copy-start.11 = (f32[5,8,128]{2,1,0:T(8,128)S(1)}, f32[5,8,128]{2,1,0:T(8,128)}, u32[]{:S(2)}) copy-start(f32[5,8,128]{2,1,0:T(8,128)} %copy-done.10) | copy-start | bytes 61444
  96.3 3.9 %copy-start.8 = (s32[64,128]{1,0:T(8,128)S(1)}, s32[64,128]{1,0:T(8,128)}, u32[]{:S(2)}) copy-start(s32[64,128]{1,0:T(8,128)} %copy-done.6) | copy-start | bytes 98308
  96.3 19.9 %copy-start.15 = (f32[1,1,4,2048]{3,2,1,0:T(4,128)S(1)}, f32[1,1,4,2048]{3,2,1,0:T(4,128)}, u32[]{:S(2)}) copy-start(f32[1,1,4,2048]{3,2,1,0:T(4,128)} %param.21) | copy-start | bytes 98308
  96.3 19.9 %copy-start.18 = (f32[4,2048]{1,0:T(4,128)S(1)}, f32[4,2048]{1,0:T(4,128)}, u32[]{:S(2)}) copy-start(f32[4,2048]{1,0:T(4,128)} %copy-done.17) | copy-start | bytes 98308
  96.3 19.9 %copy-start.20 = (f32[4,2048]{1,0:T(4,128)S(1)}, f32[4,2048]{1,0:T(4,128)}, u32[]{:S(2)}) copy-start(f32[4,2048]{1,0:T(4,128)} %copy-done.19) | copy-start | bytes 98308
  96.3 19.9 %copy-start.22 = (f32[1,1,2048]{2,1,0:T(1,128)S(1)}, f32[1,1,2048]{2,1,0:T(1,128)}, u32[]{:S(2)}) copy-start(f32[1,1,2048]{2,1,0:T(1,128)} %param.23) | copy-start | bytes 24580
  96.3 19.9 %copy-start.24 = (f32[1,1,2048]{2,1,0:T(1,128)S(1)}, f32[1,1,2048]{2,1,0:T(1,128)}, u32[]{:S(2)}) copy-start(f32[1,1,2048]{2,1,0:T(1,128)} %param.22) | copy-start | bytes 24580
  100.2 50.3 %copy-start.13 = (bf16[64,192]{1,0:T(8,128)(2,1)S(1)}, bf16[64,192]{1,0:T(8,128)(2,1)}, u32[]{:S(2)}) copy-start(bf16[64,192]{1,0:T(8,128)(2,1)} %copy-done.12) | copy-start | bytes 73732
  140.5 4.6 %collective-permute-start.16 = (f32[10,8,128]{2,1,0:T(8,128)S(1)}, f32[10,8,128]{2,1,0:T(8,128)S(1)}, u32[]{:S(2)}, u32[]{:S(2)}) collective-permute-start(f32[10,8,128]{2,1,0:T(8,128)S(1)} %columns.3.refs_4_.refs_1_), channel_id=1, source_target_pairs={{0,16},{16,32},{32,48},{48,64},{64,80},{80,96},{96,112},{112,0},{1... | collective-permute-start | bytes 122888 | tf_op jit(solution)/shard_map/ppermute | solution.py:631
  140.5 4.6 %collective-permute-start.17 = (f32[10,8,128]{2,1,0:T(8,128)S(1)}, f32[10,8,128]{2,1,0:T(8,128)S(1)}, u32[]{:S(2)}, u32[]{:S(2)}) collective-permute-start(f32[10,8,128]{2,1,0:T(8,128)S(1)} %columns.3.refs_4_.refs_1_), channel_id=1, source_target_pairs={{0,112},{16,0},{32,16},{48,32},{64,48},{80,64},{96,80},{112,96},{1... | collective-permute-start | bytes 122888 | tf_op jit(solution)/shard_map/ppermute | solution.py:631
  145.2 9.6 %collective-permute-start.18 = (f32[3,2,8,128]{3,2,1,0:T(8,128)S(1)}, f32[3,2,8,128]{3,2,1,0:T(8,128)S(1)}, u32[]{:S(2)}, u32[]{:S(2)}) collective-permute-start(f32[3,2,8,128]{3,2,1,0:T(8,128)S(1)} %edges.3), channel_id=1, source_target_pairs={{0,1},{1,2},{2,3},{3,4},{4,5},{5,6},{6,7},{7,8},{8,9},{9,10},{10,1... | collective-permute-start | bytes 73736 | tf_op jit(solution)/shard_map/ppermute | solution.py:631
  146.0 8.8 %collective-permute-start.19 = (f32[3,2,8,128]{3,2,1,0:T(8,128)S(1)}, f32[3,2,8,128]{3,2,1,0:T(8,128)S(1)}, u32[]{:S(2)}, u32[]{:S(2)}) collective-permute-start(f32[3,2,8,128]{3,2,1,0:T(8,128)S(1)} %edges.3), channel_id=1, source_target_pairs={{0,15},{1,0},{2,1},{3,2},{4,3},{5,4},{6,5},{7,6},{8,7},{9,8},{10,9... | collective-permute-start | bytes 73736 | tf_op jit(solution)/shard_map/ppermute | solution.py:631
  150.5 4.3 %copy-start.3 = (bf16[4,256,256]{2,1,0:T(8,128)(2,1)S(1)}, bf16[4,256,256]{2,1,0:T(8,128)(2,1)}, u32[]{:S(2)}) copy-start(bf16[4,256,256]{2,1,0:T(8,128)(2,1)} %copy-done.2) | copy-start | bytes 1572868
